TPU v7x, 32 devices: a 4x2x2 block of a 4x4x8 slice. The times are simulated.
32 devices in a mesh: dp: 4 (over y, z), ws: 8 (over x, core).
Axes of the slice: x: 4, y: 2, z: 2, core: 2. Of those that a mesh axis runs over, the one named last changes fastest.
The devices are a block of a 4x4x8 slice.
Arguments:
- hidden: bfloat16 [512, 768], P(('dp', 'ws')), parts along dimension 0
- self_k: bfloat16 [512, 12, 384, 64], P(('dp', 'ws')), parts along dimension 0
- self_v: bfloat16 [512, 12, 384, 64], P(('dp', 'ws')), parts along dimension 0
- cross_k: bfloat16 [512, 12, 192, 64], P(('dp', 'ws')), parts along dimension 0
- cross_v: bfloat16 [512, 12, 192, 64], P(('dp', 'ws')), parts along dimension 0
- positions: int32 [512], P(('dp', 'ws')), parts along dimension 0
- enc_mask: int32 [512, 192], P(('dp', 'ws')), parts along dimension 0
- rel_bias: float32 [12, 384], replicated
- expert_idx: int32 [512], P(('dp', 'ws')), parts along dimension 0
- ln_self: float32 [768], replicated
- ln_cross: float32 [768], replicated
- ln_ffn: float32 [768], replicated
- wq_self: bfloat16 [768, 768], P(None, 'ws')
- wk_self: bfloat16 [768, 768], P(None, 'ws')
- wv_self: bfloat16 [768, 768], P(None, 'ws')
- wo_self: bfloat16 [768, 768], P(None, 'ws')
- wq_cross: bfloat16 [768, 768], P(None, 'ws')
- wo_cross: bfloat16 [768, 768], P(None, 'ws')
- w_router: float32 [768, 8], P(None, 'ws')
- w_in: bfloat16 [8, 768, 3072], P(None, None, 'ws')
- w_out: bfloat16 [8, 3072, 768], P(None, 'ws')
Outputs:
- output 1: bfloat16 [512, 768], P(('dp', 'ws')), parts along dimension 0
- output 2: bfloat16 [512, 12, 384, 64], P(('dp', 'ws')), parts along dimension 0
- output 3: bfloat16 [512, 12, 384, 64], P(('dp', 'ws')), parts along dimension 0
There are 4 independent parts. A program takes and returns all parts, laid end to end along the dimension named above; an argument that names none is the same for every part.
All inputs are finite; a program needn't handle non-finite values.
Results may differ from a plain program's by a relative error of at most 0.0115161.
Values are sent between devices in bfloat16 or wider.
A program may use at most 768 MiB of HBM per device.

v0:
```python
import functools
import jax
import jax.numpy as jnp
from jax import lax
from jax.sharding import PartitionSpec as P

EPSILON = 1e-6
NEG_BIG = -1e30


def rms_norm(hidden, scale):
    hid_f32 = hidden.astype(jnp.float32)
    inv_rms = lax.rsqrt(jnp.mean(hid_f32 * hid_f32, axis=-1, keepdims=True) + EPSILON)
    return (hid_f32 * inv_rms * scale).astype(jnp.bfloat16)


def project(x_norm, weight):
    return jnp.dot(x_norm, weight, preferred_element_type=jnp.float32).astype(jnp.bfloat16)


def attend(queries, cache_keys, cache_vals, score_bias):
    scores = jnp.einsum('bhd,bhld->bhl', queries, cache_keys, preferred_element_type=jnp.float32) + score_bias
    attn_probs = jax.nn.softmax(scores, axis=-1).astype(jnp.bfloat16)
    context = jnp.einsum('bhl,bhld->bhd', attn_probs, cache_vals, preferred_element_type=jnp.float32)
    return context.astype(jnp.bfloat16)


def self_bias(rel_bias, positions, cache_len):
    distance = positions[:, None] - jnp.arange(cache_len)[None, :]
    pos_bias = jnp.take(rel_bias, jnp.clip(distance, 0, cache_len - 1), axis=1)
    pos_bias = jnp.where(distance[None] >= 0, pos_bias, NEG_BIG).transpose(1, 0, 2)
    return distance, pos_bias


def solution(mesh):
    ws_size = mesh.shape['ws']
    row_axes = ('dp', 'ws')
    row_vec = P(row_axes)
    row_mat = P(row_axes, None)
    cache_spec = P(row_axes, None, None, None)
    col_split = P(None, 'ws')
    in_specs = (row_mat, cache_spec, cache_spec, cache_spec, cache_spec, row_vec, row_mat, P(None, None), row_vec,
                P(None), P(None), P(None), col_split, col_split, col_split, col_split, col_split, col_split,
                col_split, P(None, None, 'ws'), P(None, 'ws', None))
    out_specs = (row_mat, cache_spec, cache_spec)

    def decoder_block(hidden, self_k, self_v, cross_k, cross_v, positions, enc_mask, rel_bias, expert_idx,
                      ln_self, ln_cross, ln_ffn, wq_self, wk_self, wv_self, wo_self, wq_cross, wo_cross,
                      w_router, w_in, w_out):
        gather_ws = functools.partial(lax.all_gather, axis_name='ws', tiled=True)
        wq_full = gather_ws(wq_self, axis=1)
        wk_full = gather_ws(wk_self, axis=1)
        wv_full = gather_ws(wv_self, axis=1)
        wo_full = gather_ws(wo_self, axis=1)
        wqc_full = gather_ws(wq_cross, axis=1)
        woc_full = gather_ws(wo_cross, axis=1)
        router_full = gather_ws(w_router, axis=1)
        win_full = gather_ws(w_in, axis=2)
        wout_full = gather_ws(w_out, axis=1)
        idx_all = gather_ws(expert_idx, axis=0)

        local_rows = hidden.shape[0]
        num_heads = rel_bias.shape[0]
        head_shape = (local_rows, num_heads, wq_full.shape[1] // num_heads)
        experts = win_full.shape[0]
        group_rows = local_rows * ws_size
        capacity = (2 * group_rows + experts - 1) // experts

        x_norm = rms_norm(hidden, ln_self)
        queries = project(x_norm, wq_full).reshape(head_shape)
        k_new = project(x_norm, wk_full).reshape(head_shape)
        v_new = project(x_norm, wv_full).reshape(head_shape)
        distance, pos_bias = self_bias(rel_bias, positions, self_k.shape[2])
        write_mask = (distance == 0)[:, None, :, None]
        new_self_k = jnp.where(write_mask, k_new[:, :, None, :], self_k)
        new_self_v = jnp.where(write_mask, v_new[:, :, None, :], self_v)
        context = attend(queries, new_self_k, new_self_v, pos_bias).reshape(local_rows, -1)
        after_self = (hidden.astype(jnp.float32) + jnp.dot(context, wo_full, preferred_element_type=jnp.float32)).astype(jnp.bfloat16)

        x_norm = rms_norm(after_self, ln_cross)
        queries = project(x_norm, wqc_full).reshape(head_shape)
        mask_bias = jnp.where(enc_mask == 1, 0.0, NEG_BIG)[:, None, :]
        context = attend(queries, cross_k, cross_v, mask_bias).reshape(local_rows, -1)
        after_cross = (after_self.astype(jnp.float32) + jnp.dot(context, woc_full, preferred_element_type=jnp.float32)).astype(jnp.bfloat16)

        x_norm = rms_norm(after_cross, ln_ffn)
        logits = jnp.dot(x_norm.astype(jnp.float32), router_full, precision=lax.Precision.HIGHEST,
                         preferred_element_type=jnp.float32)
        router_probs = jax.nn.softmax(logits, axis=-1)
        chosen = jnp.arange(experts)[None, :] == expert_idx[:, None]
        gate_val = jnp.sum(jnp.where(chosen, router_probs, 0.0), axis=-1)
        row_ids = lax.axis_index('ws') * local_rows + jnp.arange(local_rows)
        earlier = (idx_all[None, :] == expert_idx[:, None]) & (jnp.arange(group_rows)[None, :] < row_ids[:, None])
        slot_idx = jnp.sum(earlier.astype(jnp.int32), axis=1)
        keep_gate = jnp.where(slot_idx < capacity, gate_val, 0.0)
        ffn_hidden = jnp.einsum('bd,bdf->bf', x_norm, jnp.take(win_full, expert_idx, axis=0),
                                preferred_element_type=jnp.float32)
        ffn_hidden = jax.nn.relu(ffn_hidden).astype(jnp.bfloat16)
        expert_out = jnp.einsum('bf,bfd->bd', ffn_hidden, jnp.take(wout_full, expert_idx, axis=0),
                                preferred_element_type=jnp.float32).astype(jnp.bfloat16)
        hidden_out = (after_cross.astype(jnp.float32) + expert_out.astype(jnp.float32) * keep_gate[:, None]).astype(jnp.bfloat16)
        return hidden_out, new_self_k, new_self_v

    return jax.shard_map(decoder_block, mesh=mesh, in_specs=in_specs, out_specs=out_specs, check_vma=False)
```

profile of v0, /device:TPU:81, one launch (start us, length us, event | category | flops | bytes accessed | tf_op | source)
XLA Modules:
  0.0 593.6 jit_solution(1620036615121630215)
XLA Ops:
  7.3 0.7 all-gather.12.cloned.1.call-update
  8.0 0.1 all-gather.14.cloned.1.call-start
  8.1 0.7 all-gather.14.cloned.1.call-update
  8.9 0.1 all-gather.10.cloned.1.call-start
  8.9 0.7 all-gather.10.cloned.1.call-update
  9.7 0.1 all-gather.16.cloned.1.call-start
  9.7 0.6 all-gather.16.cloned.1.call-update
  10.3 0.1 all-gather.18.cloned.1.call-start
  10.4 0.6 all-gather.18.cloned.1.call-update
  11.0 0.6 all-gather.20.cloned.1.call-update
  11.6 0.7 all-gather.22.cloned.1.call-update
  12.4 0.1 all-gather.24.cloned.1.call-start
  12.5 0.7 all-gather.24.cloned.1.call-update
  13.2 0.9 copy.27
  14.1 0.7 compare_select_fusion
  14.8 21.0 %gather_fusion = f32[6144,12]{1,0:T(8,128)} fusion(f32[12,384]{0,1:T(8,128)S(1)} %copy.27, s32[6144]{0:T(1024)S(1)} %broadcast_clamp_fusion), kind=kCustom, calls=%fused_computation | custom fusion | bytes 614400 | tf_op jit(solution)/shard_map/jit(_take)/gather | solution.py:30
  35.9 0.6 dynamic-slice
  37.1 0.2 dynamic-update-slice
  37.4 8.9 %all-reduce = s32[128]{0:T(128)S(1)} all-reduce(s32[128]{0:T(128)S(1)} %dynamic-update-slice), channel_id=1, replica_groups=mesh['dp'=4,'ws'=8] {'ws'}, use_global_device_ids=true, to_apply=%add | all-reduce | flops 128 | bytes 1024
  46.3 14.9 %all-gather = f32[8,1,768]{2,1,0:T(1,128)S(1)} all-gather(f32[1,1,768]{2,1,0:T(1,128)S(1)} %bitcast.73), channel_id=1, replica_groups=mesh['dp'=4,'ws'=8] {'ws'}, dimensions={0}, use_global_device_ids=true | all-gather | bytes 27648 | tf_op jit(solution)/shard_map/all_gather | solution.py:57
  61.2 0.1 fusion.36
  61.3 0.2 convert_reduce_fusion
  61.5 0.1 fusion.49
  61.7 1.7 convolution_convert_fusion.2
  63.4 0.1 broadcast_in_dim.113
  63.6 1.7 convolution_convert_fusion.1
  65.3 0.1 broadcast_in_dim.119
  65.4 12.7 %all-gather.10.cloned.1.call-done = bf16[768,768]{0,1:T(8,128)(2,1)} async-done(((bf16[768,96]{0,1:T(8,128)(2,1)}), bf16[768,768]{0,1:T(8,128)(2,1)}) %all-gather.10.cloned.1.call-update) | async-done | bytes 1179664 | tf_op jit(solution)/shard_map/all_gather | solution.py:51
  78.1 1.7 convolution_convert_fusion.3
  79.8 0.1 reshape.256
  80.0 12.2 %broadcast_select_fusion = (bf16[16,12,384,64]{2,3,1,0:T(8,128)(2,1)}, bf16[16,12,384,64]{2,3,1,0:T(8,128)(2,1)S(1)}) fusion(bf16[16,12,384,64]{2,3,1,0:T(8,128)(2,1)} %param.23, pred[16,384]{1,0:T(8,128)(4,1)S(1)} %get-tuple-element.13, bf16[16,12,64]{2,1,0:T(8,128)(2,1)S(1)} %broadcast_in_dim.119, bf16[16,12,384,64]{2,3,1,0:T(8,128)(2,1)} %param.22, ...), kind=kLoop, calls=%fused_computation.27 | loop fusion | flops 9437184 | bytes 37804032 | tf_op jit(solution)/shard_map/jit(_where)/select_n | solution.py:76
  92.2 3.7 copy-done
  95.9 1.7 fusion.70
  97.7 1.1 copy.29
  98.8 5.1 fusion.18
  103.8 2.3 copy.30
  106.1 7.0 %fusion.71 = bf16[16,12,1,64]{3,2,1,0:T(2,128)(2,1)S(1)} fusion(bf16[16,12,384,1]{2,3,1,0:T(2,128)(2,1)S(1)} %copy.30, bf16[16,12,384,64]{2,3,1,0:T(8,128)(2,1)} %get-tuple-element.9), kind=kOutput, calls=%fused_computation.116 | convolution fusion | flops 9437184 | bytes 9609216 | tf_op jit(solution)/shard_map/bhl,bhld->bhd/dot_general | solution.py:24
  113.2 0.1 reshape.168
  113.3 1.8 multiply_reduce_fusion.1
  115.1 6.4 %all-gather.18.cloned.1.call-done = bf16[768,768]{0,1:T(8,128)(2,1)} async-done(((bf16[768,96]{0,1:T(8,128)(2,1)}), bf16[768,768]{0,1:T(8,128)(2,1)}) %all-gather.18.cloned.1.call-update) | async-done | bytes 1179664 | tf_op jit(solution)/shard_map/all_gather | solution.py:55
  121.5 1.7 convolution_convert_fusion
  123.2 0.1 reshape.258
  123.4 3.7 fusion.72
  127.1 0.2 fusion.23
  127.3 4.5 fusion.31
  131.8 0.1 reshape.170
  132.0 11.4 %all-gather.20.cloned.1.call-done = bf16[768,768]{0,1:T(8,128)(2,1)} async-done(((bf16[768,96]{0,1:T(8,128)(2,1)}), bf16[768,768]{0,1:T(8,128)(2,1)}) %all-gather.20.cloned.1.call-update) | async-done | bytes 1179664 | tf_op jit(solution)/shard_map/all_gather | solution.py:56
  143.3 1.8 multiply_reduce_fusion
  145.2 0.2 fusion.69
  145.5 0.5 compare_select_fusion.4
  146.0 0.1 fusion.63
  146.1 171.3 %all-gather.22.cloned.1.call-done = bf16[8,768,3072]{2,1,0:T(8,128)(2,1)} async-done(((bf16[8,768,384]{2,1,0:T(8,128)(2,1)}), bf16[8,768,3072]{2,1,0:T(8,128)(2,1)}) %all-gather.22.cloned.1.call-update) | async-done | bytes 37748752 | tf_op jit(solution)/shard_map/all_gather | solution.py:58
  317.4 24.4 %fusion.67 = (bf16[8,768,1024]{2,1,0:T(8,128)(2,1)}, bf16[8,768,1024]{2,1,0:T(8,128)(2,1)}, bf16[8,768,1024]{2,1,0:T(8,128)(2,1)}) fusion(bf16[8,768,3072]{2,1,0:T(8,128)(2,1)} %all-gather.22.cloned.1.call-done), kind=kLoop, calls=%fused_computation.112 | loop fusion | bytes 75497472 | tf_op jit(solution)/shard_map/jit(_take)/gather | solution.py:96
  341.8 14.5 %gather_fusion.1 = bf16[16,768,1024]{2,1,0:T(8,128)(2,1)} fusion(bf16[8,768,1024]{2,1,0:T(8,128)(2,1)} %get-tuple-element.3, s32[1024]{0:T(1024)S(1)} %pad_clamp_fusion), kind=kCustom, calls=%fused_computation.1 | custom fusion | bytes 50331712 | tf_op jit(solution)/shard_map/jit(_take)/gather | solution.py:96
  356.4 14.6 %gather_fusion.2 = bf16[16,768,1024]{2,1,0:T(8,128)(2,1)} fusion(bf16[8,768,1024]{2,1,0:T(8,128)(2,1)} %get-tuple-element.4, s32[1024]{0:T(1024)S(1)} %pad_clamp_fusion), kind=kCustom, calls=%fused_computation.2 | custom fusion | bytes 50331712 | tf_op jit(solution)/shard_map/jit(_take)/gather | solution.py:96
  371.0 14.6 %gather_fusion.3 = bf16[16,768,1024]{2,1,0:T(8,128)(2,1)} fusion(bf16[8,768,1024]{2,1,0:T(8,128)(2,1)} %get-tuple-element.5, s32[1024]{0:T(1024)S(1)} %pad_clamp_fusion), kind=kCustom, calls=%fused_computation.3 | custom fusion | bytes 50331712 | tf_op jit(solution)/shard_map/jit(_take)/gather | solution.py:96
  385.6 27.4 %fusion.4 = bf16[16,1,3072]{2,1,0:T(2,128)(2,1)S(1)} fusion(bf16[16,768,1024]{2,1,0:T(8,128)(2,1)} %gather_fusion.3, bf16[16,768,1024]{2,1,0:T(8,128)(2,1)} %gather_fusion.2, bf16[16,768,1024]{2,1,0:T(8,128)(2,1)} %gather_fusion.1, pred[16]{0:T(512)(128)(4,1)S(1)} %compare_and_fusion, bf16[16,768,1]{1,0,2:T(8,128)(2,1)S(1)} %fusion.63), kind=kOutput, calls=%fused_computation.12 | convolution fusion | flops 339738624 | bytes 75620368 | tf_op jit(solution)/shard_map/bd,bdf->bf/dot_general | solution.py:96
  413.0 78.3 %all-gather.24.cloned.1.call-done = bf16[8,3072,768]{2,1,0:T(8,128)(2,1)} async-done(((bf16[8,384,768]{2,1,0:T(8,128)(2,1)}), bf16[8,3072,768]{2,1,0:T(8,128)(2,1)}) %all-gather.24.cloned.1.call-update) | async-done | bytes 37748752 | tf_op jit(solution)/shard_map/all_gather | solution.py:59
  491.3 25.5 %fusion.68 = (bf16[8,1024,768]{2,1,0:T(8,128)(2,1)}, bf16[8,1024,768]{2,1,0:T(8,128)(2,1)}, bf16[8,1024,768]{2,1,0:T(8,128)(2,1)}) fusion(bf16[8,3072,768]{2,1,0:T(8,128)(2,1)} %all-gather.24.cloned.1.call-done), kind=kLoop, calls=%fused_computation.113 | loop fusion | bytes 75497472 | tf_op jit(solution)/shard_map/jit(_take)/gather | solution.py:99
  516.8 14.6 %gather_fusion.4 = bf16[16,1024,768]{2,1,0:T(8,128)(2,1)} fusion(bf16[8,1024,768]{2,1,0:T(8,128)(2,1)} %get-tuple-element.6, s32[1024]{0:T(1024)S(1)} %pad_clamp_fusion), kind=kCustom, calls=%fused_computation.4 | custom fusion | bytes 50331712 | tf_op jit(solution)/shard_map/jit(_take)/gather | solution.py:99
  531.4 14.6 %gather_fusion.5 = bf16[16,1024,768]{2,1,0:T(8,128)(2,1)} fusion(bf16[8,1024,768]{2,1,0:T(8,128)(2,1)} %get-tuple-element.7, s32[1024]{0:T(1024)S(1)} %pad_clamp_fusion), kind=kCustom, calls=%fused_computation.5 | custom fusion | bytes 50331712 | tf_op jit(solution)/shard_map/jit(_take)/gather | solution.py:99
  545.9 14.6 %gather_fusion.6 = bf16[16,1024,768]{2,1,0:T(8,128)(2,1)} fusion(bf16[8,1024,768]{2,1,0:T(8,128)(2,1)} %get-tuple-element.8, s32[1024]{0:T(1024)S(1)} %pad_clamp_fusion), kind=kCustom, calls=%fused_computation.6 | custom fusion | bytes 50331712 | tf_op jit(solution)/shard_map/jit(_take)/gather | solution.py:99
  560.5 25.6 %fusion.9 = bf16[16,1,768]{2,1,0:T(2,128)(2,1)S(1)} fusion(bf16[16,1024,768]{2,1,0:T(8,128)(2,1)} %gather_fusion.6, bf16[16,1024,768]{2,1,0:T(8,128)(2,1)} %gather_fusion.5, bf16[16,1024,768]{2,1,0:T(8,128)(2,1)} %gather_fusion.4, pred[16]{0:T(512)(128)(4,1)S(1)} %compare_and_fusion, bf16[16,3072,1]{1,0,2:T(8,128)(2,1)S(1)} %fusion.34), kind=kOutput, calls=%fused_computation.18 | convolution fusion | flops 339738624 | bytes 75620368 | tf_op jit(solution)/shard_map/bf,bfd->bd/dot_general | solution.py:99
  586.1 0.7 add_convert_fusion
  (47 shorter events, 0.5 us)
Async XLA Ops:
  7.2 28.7 %copy-start.12 = (u32[32]{0:T(128)S(1)}, u32[32]{0:T(128)}, u32[]{:S(2)}) copy-start(u32[32]{0:T(128)} %constant.85) | copy-start | bytes 388
  7.2 54.3 %copy-start.9 = (s32[16]{0:T(128)S(1)}, s32[16]{0:T(128)}, u32[]{:S(2)}) copy-start(s32[16]{0:T(128)} %param.26) | copy-start | bytes 196
  7.2 29.9 %copy-start.10 = (s32[16]{0:T(128)S(1)}, s32[16]{0:T(128)}, u32[]{:S(2)}) copy-start(s32[16]{0:T(128)} %param.29) | copy-start | bytes 196
  7.2 39.1 %copy-start.8 = (f32[768,1]{0,1:T(1,128)S(1)}, f32[768,1]{0,1:T(1,128)}, u32[]{:S(2)}) copy-start(f32[768,1]{0,1:T(1,128)} %param.39) | copy-start | bytes 9220
  7.2 54.0 %copy-start.3 = (bf16[16,768]{1,0:T(8,128)(2,1)S(1)}, bf16[16,768]{1,0:T(8,128)(2,1)}, u32[]{:S(2)}) copy-start(bf16[16,768]{1,0:T(8,128)(2,1)} %param.21) | copy-start | bytes 73732
  7.2 54.4 %copy-start.5 = (s32[16,192]{1,0:T(8,128)S(1)}, s32[16,192]{1,0:T(8,128)}, u32[]{:S(2)}) copy-start(s32[16,192]{1,0:T(8,128)} %param.27) | copy-start | bytes 36868
  7.2 54.4 %copy-start.4 = (f32[768]{0:T(1024)S(1)}, f32[768]{0:T(1024)}, u32[]{:S(2)}) copy-start(f32[768]{0:T(1024)} %param.30) | copy-start | bytes 9220
  7.3 54.4 %all-gather.12.cloned.1.call-start = ((), (), s32[]{:S(2)}) async-start(), calls=%async_computation.1 | async-start | bytes 1327104 | tf_op jit(solution)/shard_map/all_gather | solution.py:52
  8.0 55.5 %all-gather.14.cloned.1.call-start = ((), (), s32[]{:S(2)}) async-start(), calls=%async_computation.2 | async-start | bytes 1327104 | tf_op jit(solution)/shard_map/all_gather | solution.py:53
  8.9 69.3 %all-gather.10.cloned.1.call-start = ((), (), s32[]{:S(2)}) async-start(), calls=%async_computation | async-start | bytes 1327104 | tf_op jit(solution)/shard_map/all_gather | solution.py:51
  9.7 103.6 %all-gather.16.cloned.1.call-start = ((), (), s32[]{:S(2)}) async-start(), calls=%async_computation.3 | async-start | bytes 1327104 | tf_op jit(solution)/shard_map/all_gather | solution.py:54
  10.3 111.2 %all-gather.18.cloned.1.call-start = ((), (), s32[]{:S(2)}) async-start(), calls=%async_computation.4 | async-start | bytes 1327104 | tf_op jit(solution)/shard_map/all_gather | solution.py:55
  10.9 132.4 %all-gather.20.cloned.1.call-start = ((), (), s32[]{:S(2)}) async-start(), calls=%async_computation.5 | async-start | bytes 1327104 | tf_op jit(solution)/shard_map/all_gather | solution.py:56
  11.6 305.8 %all-gather.22.cloned.1.call-start = ((), (), s32[]{:S(2)}) async-start(), calls=%async_computation.6 | async-start | bytes 42467328 | tf_op jit(solution)/shard_map/all_gather | solution.py:58
  12.4 478.9 %all-gather.24.cloned.1.call-start = ((), (), s32[]{:S(2)}) async-start(), calls=%async_computation.7 | async-start | bytes 42467328 | tf_op jit(solution)/shard_map/all_gather | solution.py:59
  92.2 3.7 copy-start
  98.8 22.8 %copy-start.7 = (f32[768]{0:T(1024)S(1)}, f32[768]{0:T(1024)}, u32[]{:S(2)}) copy-start(f32[768]{0:T(1024)} %param.31) | copy-start | bytes 9220
  113.1 32.1 %copy-start.6 = (f32[768]{0:T(1024)S(1)}, f32[768]{0:T(1024)}, u32[]{:S(2)}) copy-start(f32[768]{0:T(1024)} %param.32) | copy-start | bytes 9220
  145.2 0.8 copy-start.1
  560.5 25.6 %copy-start.2 = (f32[16,768]{1,0:T(8,128)S(1)}, f32[16,768]{1,0:T(8,128)}, u32[]{:S(2)}) copy-start(f32[16,768]{1,0:T(8,128)} %copy-done.1) | copy-start | bytes 147460
  560.5 25.6 %copy-start.11 = (f32[16]{0:T(128)S(1)}, f32[16]{0:T(128)}, u32[]{:S(2)}) copy-start(f32[16]{0:T(128)} %compare_select_fusion.4) | copy-start | bytes 196
Sparse Core Ops, SparseCore 0:
  9.7 24.7 all-gather.11
  36.0 20.2 all-gather.13
  57.9 20.1 all-gather.9
  79.6 20.2 all-gather.15
  101.3 20.2 all-gather.17
  123.0 20.3 all-gather.19
  145.0 172.3 all-gather.21
  319.0 172.2 all-gather.23
where the time goes:
time: 594 us
  waiting for transfers between devices  285 us (48%)
  local copies, waits for them, and re-layouts  168 us (28%)
  matrix products  80.6 us (14%)
  blocking collectives  23.8 us (4%)
  other arithmetic  20.1 us (3%)
  between operations  15.2 us (3%)
    all_gather x1, waiting for transfers between devices, decoder_block(): win_full = gather_ws(w_in, axis=2)  171 us
    all_gather x1, waiting for transfers between devices, decoder_block(): wout_full = gather_ws(w_out, axis=1)  78.3 us
    gather x4, local copies, waits for them, and re-layouts, decoder_block(): jnp.take(wout_full, expert_idx, axis=0)  69.2 us
    gather x4, local copies, waits for them, and re-layouts, decoder_block(): jnp.take(win_full, expert_idx, axis=0)  68.2 us
    dot_general x1, matrix products, decoder_block(): jnp.einsum('bd,bdf->bf', x_norm, jnp.take(win_full, expert_idx, axis=0),...  27.4 us
    dot_general x1, matrix products, decoder_block(): jnp.einsum('bf,bfd->bd', ffn_hidden, jnp.take(wout_full, expert_idx, axis...  25.6 us
    gather x1, local copies, waits for them, and re-layouts, self_bias(): pos_bias = jnp.take(rel_bias, jnp.clip(distance, 0, cache_len - 1), axis=1)  21 us
    all_gather x1, blocking collectives, decoder_block(): router_full = gather_ws(w_router, axis=1)  14.9 us
  transfers between devices with their start and end apart: 8, of which 5 were waited for; matrix products, arithmetic and copies ran while one was open for 29% of the time, Pallas kernels for 0%

commit v1 on v0

v1 whole, which is shorter than its diff:
```python
import functools
import jax
import jax.numpy as jnp
from jax import lax
from jax.experimental import pallas as pl
from jax.experimental.pallas import tpu as pltpu
from jax.sharding import PartitionSpec as P

EPSILON = 1e-6
NEG_BIG = -1e30
F32, BF16 = jnp.float32, jnp.bfloat16
MESH = pl.DeviceIdType.MESH
ANY = pl.BlockSpec(memory_space=pl.ANY)
VM = pl.BlockSpec(memory_space=pltpu.VMEM)
HBM = pl.BlockSpec(memory_space=pltpu.HBM)
SM = pl.BlockSpec(memory_space=pltpu.SMEM)
NT = (((1,), (1,)), ((), ()))
PEERS = ((2, 0), (2, 1), (1, 0), (3, 0), (1, 1), (3, 1), (0, 1))
UNROLL = 4


def rms_norm(hid_f32, scale):
    inv_rms = lax.rsqrt(jnp.mean(hid_f32 * hid_f32, axis=-1, keepdims=True) + EPSILON)
    return (hid_f32 * inv_rms * scale).astype(BF16)


def dot_nt(a, b):
    return lax.dot_general(a, b, NT, preferred_element_type=F32)


def softmax_rows(scores):
    top = jnp.max(scores, axis=-1, keepdims=True)
    ex = jnp.exp(scores - top)
    return (ex / jnp.sum(ex, axis=-1, keepdims=True)).astype(BF16)


def make_dev(n):
    me = lax.axis_index('ws')
    chips = n // 2
    chip, core = me // 2, lax.rem(me, 2)

    def dev(step, other):
        return 2 * lax.rem(chip + step, chips) + ((1 - core) if other else core)
    return me, dev


def remote(src, dst, send_sem, recv_sem, dev):
    return pltpu.make_async_remote_copy(src_ref=src, dst_ref=dst, send_sem=send_sem, recv_sem=recv_sem,
                                        device_id={'ws': dev}, device_id_type=MESH)


def head_mask(heads_pad, width, head_dim):
    row = lax.broadcasted_iota(jnp.int32, (heads_pad, width), 0)
    col = lax.broadcasted_iota(jnp.int32, (heads_pad, width), 1)
    return (col // head_dim == row).astype(F32)


def proj_kernel(n, hid_hbm, ln_hbm, wq_hbm, wk_hbm, wv_hbm, wo_hbm, wqc_hbm, woc_hbm, k_hbm, v_hbm, ck_hbm, cv_hbm,
                qkv_ref, wall_ref, k_ref, v_ref, ck_ref, cv_ref,
                xall_ref, ln_ref, wqkv_ref, qsend_ref, qrecv_ref,
                in_sem, big_sem, x_send, x_recv, q_send, q_recv, w_send, w_recv):
    me, dev = make_dev(n)
    rows, width = hid_hbm.shape
    share = width // n
    half = share // 2
    piece = share + half

    barrier = pltpu.get_barrier_semaphore()
    for peer in PEERS:
        pl.semaphore_signal(barrier, inc=1, device_id={'ws': dev(*peer)}, device_id_type=MESH)

    mine = wall_ref.at[me]
    loads = [
        (hid_hbm, xall_ref.at[me]), (ln_hbm, ln_ref), (wq_hbm, wqkv_ref.at[0]), (wk_hbm, wqkv_ref.at[1]),
        (wv_hbm, wqkv_ref.at[2]),
        (wo_hbm, mine.at[pl.ds(0, share)]), (woc_hbm.at[pl.ds(0, half)], mine.at[pl.ds(share, half)]),
        (wqc_hbm, mine.at[pl.ds(piece, share)]),
        (woc_hbm.at[pl.ds(half, half)], mine.at[pl.ds(piece + share, half)]),
    ]
    loads = [pltpu.make_async_copy(src, dst, in_sem.at[i]) for i, (src, dst) in enumerate(loads)]
    for load in loads:
        load.start()
    big = [pltpu.make_async_copy(src, dst, big_sem.at[i]) for i, (src, dst) in
           enumerate([(k_hbm, k_ref), (v_hbm, v_ref), (ck_hbm, ck_ref), (cv_hbm, cv_ref)])]

    loads[0].wait()
    pl.semaphore_wait(barrier, n - 1)
    x_out = [remote(xall_ref.at[me], xall_ref.at[me], x_send.at[i], x_recv.at[me], dev(*peer))
             for i, peer in enumerate(PEERS)]
    for copy in x_out:
        copy.start()

    right, left, far, sib = dev(1, 0), dev(3, 0), dev(2, 0), dev(0, 1)
    w_out = []

    def send_piece(owner, part, target):
        block = wall_ref.at[owner, pl.ds(part * piece, piece)]
        copy = remote(block, block, w_send.at[len(w_out)], w_recv.at[owner, part], target)
        copy.start()
        w_out.append(copy)

    def wait_piece(owner, part):
        block = wall_ref.at[owner, pl.ds(part * piece, piece)]
        remote(block, block, w_send.at[0], w_recv.at[owner, part], sib).wait_recv()

    for load in loads[5:]:
        load.wait()
    send_piece(me, 0, right)
    send_piece(me, 1, left)
    for load in big:
        load.start()
    qsend_ref[...] = jnp.zeros_like(qsend_ref)

    for load in loads[1:5]:
        load.wait()
    for peer in PEERS:
        src = dev(*peer)
        remote(xall_ref.at[src], xall_ref.at[src], x_send.at[0], x_recv.at[src], src).wait_recv()
    x_norm = rms_norm(xall_ref[...].reshape(n * rows, width).astype(F32), ln_ref[...])
    for part in range(3):
        qsend_ref[:, part * 128:part * 128 + share] = dot_nt(x_norm, wqkv_ref[part]).astype(BF16)
    q_out = []
    for i, peer in enumerate(PEERS):
        dst = dev(*peer)
        q_out.append(remote(qsend_ref.at[pl.ds(dst * rows, rows)], qrecv_ref.at[me], q_send.at[i], q_recv.at[me], dst))
    for copy in q_out:
        copy.start()
    qrecv_ref[me] = qsend_ref[pl.ds(pl.multiple_of(me * rows, rows), rows), :]
    send_piece(me, 1, right)
    send_piece(me, 0, left)
    send_piece(me, 0, sib)
    send_piece(me, 1, sib)

    wait_piece(left, 0)
    send_piece(left, 0, right)
    wait_piece(right, 1)
    send_piece(right, 1, left)
    send_piece(left, 0, sib)
    send_piece(right, 1, sib)

    for peer in PEERS:
        src = dev(*peer)
        remote(qrecv_ref.at[src], qrecv_ref.at[src], q_send.at[0], q_recv.at[src], src).wait_recv()
    for part in range(3):
        qkv_ref[part] = jnp.concatenate([qrecv_ref[s][:, part * 128:part * 128 + share] for s in range(n)],
                                        axis=1).astype(F32)

    wait_piece(left, 1)
    send_piece(left, 1, sib)
    wait_piece(right, 0)
    send_piece(right, 0, sib)
    wait_piece(far, 0)
    send_piece(far, 0, sib)
    wait_piece(far, 1)
    send_piece(far, 1, sib)
    for step in range(n // 2):
        src = dev(step, 1)
        wait_piece(src, 0)
        wait_piece(src, 1)
    for load in big:
        load.wait()
    for copy in x_out + q_out + w_out:
        copy.wait_send()


def self_kernel(head_dim, pos_ref, qkv_ref, rel_ref, k_ref, v_ref, win_hbm, wout_hbm,
                newk_hbm, newv_hbm, ctx_ref, win_ref, wout_ref,
                kt_ref, vt_ref, kp_ref, vp_ref, s_ref, p_ref, ctx32_ref, rrev_ref, w_sem, k_sem, v_sem):
    rows, width, length = k_ref.shape
    heads_pad = s_ref.shape[1]
    steps = rows // UNROLL
    tiles = length // 128
    w_loads = [pltpu.make_async_copy(win_hbm, win_ref, w_sem.at[0]),
               pltpu.make_async_copy(wout_hbm, wout_ref, w_sem.at[1])]

    rel = jnp.concatenate([rel_ref[...], jnp.zeros((heads_pad - rel_ref.shape[0], length), F32)], axis=0)
    flip = (lax.broadcasted_iota(jnp.int32, (length, length), 0) + lax.broadcasted_iota(jnp.int32, (length, length), 1)
            == length - 1).astype(F32).astype(BF16)
    hi = rel.astype(BF16)
    rest = rel - hi.astype(F32)
    mid = rest.astype(BF16)
    low = (rest - mid.astype(F32)).astype(BF16)
    rrev_ref[...] = (jnp.dot(hi, flip, preferred_element_type=F32) + jnp.dot(mid, flip, preferred_element_type=F32)
                     + jnp.dot(low, flip, preferred_element_type=F32))
    pad = jnp.zeros((128 - rows, width), F32)
    kt_ref[...] = jnp.concatenate([qkv_ref[1], pad], axis=0).T
    vt_ref[...] = jnp.concatenate([qkv_ref[2], pad], axis=0).T

    h_mask = head_mask(heads_pad, width, head_dim)
    lane = lax.broadcasted_iota(jnp.int32, (1, length), 1)
    lane_tile = lax.broadcasted_iota(jnp.int32, (1, 128), 1)

    def out_copies(b, old_ref, patch_ref, new_hbm, sem):
        tile = pos_ref[b] // 128
        copies = []
        for k in range(tiles):
            cols = pl.ds(pl.multiple_of(lax.rem(tile + k, tiles) * 128, 128), 128)
            src = patch_ref.at[b] if k == 0 else old_ref.at[b, :, cols]
            copies.append(pltpu.make_async_copy(src, new_hbm.at[b, :, cols], sem.at[b, k]))
        return copies

    def put_row(b, column, old_ref, patch_ref, new_hbm, sem):
        pos = pos_ref[b]
        first = pl.multiple_of(pos // 128 * 128, 128)
        patch_ref[b] = jnp.where(lane_tile == pos - first, jnp.broadcast_to(column, (width, 128)).astype(BF16),
                                 old_ref[b, :, pl.ds(first, 128)])
        for copy in out_copies(b, old_ref, patch_ref, new_hbm, sem):
            copy.start()

    def score_step(i, carry):
        kt = kt_ref[...]
        for s in range(UNROLL):
            b = i * UNROLL + s
            put_row(b, kt[:, s:s + 1], k_ref, kp_ref, newk_hbm, k_sem)
            pos = pos_ref[b]
            q_diag = qkv_ref[0, pl.ds(b, 1), :] * h_mask
            scores = jnp.dot(q_diag.astype(BF16), k_ref[b], preferred_element_type=F32)
            new = jnp.sum(q_diag * qkv_ref[1, pl.ds(b, 1), :], axis=1, keepdims=True)
            bias = pltpu.roll(rrev_ref[...], pos + 1, axis=1)
            s_ref[b] = jnp.where(lane <= pos, jnp.where(lane == pos, new, scores) + bias, NEG_BIG)
        kt_ref[...] = pltpu.roll(kt, 128 - UNROLL, axis=1)
        return carry
    lax.fori_loop(0, steps, score_step, 0)
    for load in w_loads:
        load.start()

    p_ref[...] = softmax_rows(s_ref[...])

    def value_step(i, carry):
        vt = vt_ref[...]
        for s in range(UNROLL):
            b = i * UNROLL + s
            put_row(b, vt[:, s:s + 1], v_ref, vp_ref, newv_hbm, v_sem)
            here = lane == pos_ref[b]
            probs = p_ref[b].astype(F32)
            new = jnp.sum(jnp.where(here, probs, 0.0), axis=1, keepdims=True)
            spread = dot_nt(jnp.where(here, 0.0, probs).astype(BF16), v_ref[b])
            spread = spread + new * qkv_ref[2, pl.ds(b, 1), :]
            ctx32_ref[pl.ds(b, 1), :] = jnp.sum(spread * h_mask, axis=0, keepdims=True)
        vt_ref[...] = pltpu.roll(vt, 128 - UNROLL, axis=1)
        return carry
    lax.fori_loop(0, steps, value_step, 0)
    ctx_ref[...] = ctx32_ref[...].astype(BF16)

    def drain(b, carry):
        for copy in (out_copies(b, k_ref, kp_ref, newk_hbm, k_sem) + out_copies(b, v_ref, vp_ref, newv_hbm, v_sem)):
            copy.wait()
        return carry
    lax.fori_loop(0, rows, drain, 0)
    for load in w_loads:
        load.wait()


def cross_kernel(n, head_dim, capacity, eidx_ref, ctx_ref, wall_ref, hid_hbm, lnc_hbm, lnf_hbm, mask_hbm, wr_hbm,
                 k_ref, v_ref, win_ref, wout_ref,
                 out_ref,
                 hid_ref, lnc_ref, lnf_ref, mask_ref, wr_ref, eall_ref, q_ref, s_ref,
                 p_ref, ctx32_ref, xall_ref, u_ref, part_ref, rs_ref,
                 in_sem, r_send, r_recv, e_send, e_recv, x_send, x_recv, rs_send, rs_recv):
    me, dev = make_dev(n)
    rows, width, length = k_ref.shape
    heads_pad = s_ref.shape[1]
    share = width // n
    half = share // 2
    piece = share + half
    steps = rows // UNROLL
    experts = win_ref.shape[0]

    barrier = pltpu.get_barrier_semaphore()
    for peer in PEERS:
        pl.semaphore_signal(barrier, inc=1, device_id={'ws': dev(*peer)}, device_id_type=MESH)
    loads = [(hid_hbm, hid_ref), (lnc_hbm, lnc_ref), (lnf_hbm, lnf_ref), (mask_hbm, mask_ref), (wr_hbm, wr_ref.at[me])]
    loads = [pltpu.make_async_copy(src, dst, in_sem.at[i]) for i, (src, dst) in enumerate(loads)]
    for load in loads:
        load.start()

    row_id = lax.broadcasted_iota(jnp.int32, (rows, 128), 0)
    e_own = jnp.zeros((rows, 128), jnp.int32)
    for b in range(rows):
        e_own = jnp.where(row_id == b, eidx_ref[b], e_own)
    eall_ref[me] = e_own

    loads[0].wait()
    wo = wall_ref[:, 0:share, :].reshape(width, width)
    h1 = (hid_ref[...].astype(F32) + dot_nt(ctx_ref[...], wo)).astype(BF16).astype(F32)
    loads[1].wait()
    wqc = wall_ref[:, piece:piece + share, :].reshape(width, width)
    q_ref[...] = dot_nt(rms_norm(h1, lnc_ref[...]), wqc).astype(BF16).astype(F32)

    loads[4].wait()
    pl.semaphore_wait(barrier, n - 1)
    sends = []
    for i, peer in enumerate(PEERS):
        dst = dev(*peer)
        sends.append(remote(wr_ref.at[me], wr_ref.at[me], r_send.at[i], r_recv.at[me], dst))
        sends.append(remote(eall_ref.at[me], eall_ref.at[me], e_send.at[i], e_recv.at[me], dst))
    for copy in sends:
        copy.start()

    h_mask = head_mask(heads_pad, width, head_dim)
    loads[3].wait()

    def score_step(i, carry):
        for s in range(UNROLL):
            b = i * UNROLL + s
            q_diag = (q_ref[pl.ds(b, 1), :] * h_mask).astype(BF16)
            scores = jnp.dot(q_diag, k_ref[b], preferred_element_type=F32)
            s_ref[b] = jnp.where(mask_ref[pl.ds(b, 1), :] == 1, scores, NEG_BIG)
        return carry
    lax.fori_loop(0, steps, score_step, 0)
    p_ref[...] = softmax_rows(s_ref[...])

    def value_step(i, carry):
        for s in range(UNROLL):
            b = i * UNROLL + s
            spread = dot_nt(p_ref[b], v_ref[b])
            ctx32_ref[pl.ds(b, 1), :] = jnp.sum(spread * h_mask, axis=0, keepdims=True)
        return carry
    lax.fori_loop(0, steps, value_step, 0)

    woc = jnp.concatenate([wall_ref[:, share:piece, :], wall_ref[:, piece + share:2 * piece, :]], axis=1)
    woc = woc.reshape(width, width)
    h2 = (h1 + dot_nt(ctx32_ref[...].astype(BF16), woc)).astype(BF16).astype(F32)
    loads[2].wait()
    x_own = rms_norm(h2, lnf_ref[...])
    xall_ref[me] = x_own
    x_out = [remote(xall_ref.at[me], xall_ref.at[me], x_send.at[i], x_recv.at[me], dev(*peer))
             for i, peer in enumerate(PEERS)]
    for copy in x_out:
        copy.start()

    for peer in PEERS:
        src = dev(*peer)
        remote(wr_ref.at[src], wr_ref.at[src], r_send.at[0], r_recv.at[src], src).wait_recv()
        remote(eall_ref.at[src], eall_ref.at[src], e_send.at[0], e_recv.at[src], src).wait_recv()
    x_f32 = x_own.astype(F32)
    logits = [jnp.sum(x_f32 * wr_ref[e], axis=-1, keepdims=True) for e in range(experts)]
    top = functools.reduce(jnp.maximum, logits)
    ex = [jnp.exp(v - top) for v in logits]
    total = functools.reduce(jnp.add, ex)
    e_col = e_own[:, 0:1]
    gate = functools.reduce(jnp.add, [jnp.where(e_col == e, ex[e], 0.0) for e in range(experts)]) / total
    e_all = eall_ref[...].reshape(n * rows, 128)
    one_hot = (e_all == lax.broadcasted_iota(jnp.int32, (n * rows, 128), 1)).astype(F32).astype(BF16)
    earlier = (lax.broadcasted_iota(jnp.int32, (rows, n * rows), 1)
               < me * rows + lax.broadcasted_iota(jnp.int32, (rows, n * rows), 0)).astype(F32).astype(BF16)
    counts = jnp.dot(earlier, one_hot, preferred_element_type=F32)
    slot = jnp.sum(jnp.where(lax.broadcasted_iota(jnp.int32, (rows, 128), 1) == e_own, counts, 0.0), axis=-1,
                   keepdims=True)
    keep_gate = jnp.where(slot < capacity, gate, 0.0)

    for peer in PEERS:
        src = dev(*peer)
        remote(xall_ref.at[src], xall_ref.at[src], x_send.at[0], x_recv.at[src], src).wait_recv()
    x_all = xall_ref[...].reshape(n * rows, width)
    e_wide = jnp.concatenate([e_all] * (win_ref.shape[2] // 128), axis=1)

    def expert_step(e, carry):
        u = jnp.maximum(jnp.dot(x_all, win_ref[e], preferred_element_type=F32), 0.0)
        u_ref[e] = jnp.where(e_wide == e, u, 0.0).astype(BF16)
        return carry
    lax.fori_loop(0, experts, expert_step, 0)

    chunk = part_ref.shape[2]
    rs_out = []
    for c in range(width // chunk):
        acc = jnp.zeros((n * rows, chunk), F32)
        for e in range(experts):
            acc = acc + jnp.dot(u_ref[e], wout_ref[e, :, c * chunk:(c + 1) * chunk], preferred_element_type=F32)
        part_ref[c] = acc
        rs_ref[me, c] = part_ref[c, pl.ds(pl.multiple_of(me * rows, rows), rows), :]
        for i, peer in enumerate(PEERS):
            dst = dev(*peer)
            copy = remote(part_ref.at[c, pl.ds(dst * rows, rows)], rs_ref.at[me, c], rs_send.at[c, i],
                          rs_recv.at[c, me], dst)
            copy.start()
            rs_out.append(copy)
    for c in range(width // chunk):
        for peer in PEERS:
            src = dev(*peer)
            remote(rs_ref.at[src, c], rs_ref.at[src, c], rs_send.at[c, 0], rs_recv.at[c, src], src).wait_recv()
        y = jnp.sum(rs_ref[:, c], axis=0).astype(BF16).astype(F32)
        cols = slice(c * chunk, (c + 1) * chunk)
        out_ref[:, cols] = (h2[:, cols] + y * keep_gate).astype(BF16)
    for copy in sends + x_out + rs_out:
        copy.wait_send()


def solution(mesh):
    n = mesh.shape['ws']
    row_axes = ('dp', 'ws')
    row_vec = P(row_axes)
    row_mat = P(row_axes, None)
    cache_spec = P(row_axes, None, None, None)
    col_split = P(None, 'ws')
    in_specs = (row_mat, cache_spec, cache_spec, cache_spec, cache_spec, row_vec, row_mat, P(None, None), row_vec,
                P(None), P(None), P(None), col_split, col_split, col_split, col_split, col_split, col_split,
                col_split, P(None, None, 'ws'), P(None, 'ws', None))
    out_specs = (row_mat, cache_spec, cache_spec)

    def decoder_block(hidden, self_k, self_v, cross_k, cross_v, positions, enc_mask, rel_bias, expert_idx,
                      ln_self, ln_cross, ln_ffn, wq_self, wk_self, wv_self, wo_self, wq_cross, wo_cross,
                      w_router, w_in, w_out):
        rows, width = hidden.shape
        heads, length, head_dim = self_k.shape[1:]
        src_len = cross_k.shape[2]
        share = width // n
        heads_pad = -(-heads // 16) * 16
        experts, _, units = w_in.shape
        capacity = (2 * rows * n + experts - 1) // experts
        chunk = 256

        def flat(cache):
            return jnp.swapaxes(cache, 2, 3).reshape(rows, width, cache.shape[2])

        dma = pltpu.SemaphoreType.DMA
        qkv, wall, kv_k, kv_v, c_k, c_v = pl.pallas_call(
            functools.partial(proj_kernel, n),
            out_shape=(pltpu.VMEM((3, rows, width), F32), pltpu.VMEM((n, 3 * share, width), BF16),
                       pltpu.VMEM((rows, width, length), BF16), pltpu.VMEM((rows, width, length), BF16),
                       pltpu.VMEM((rows, width, src_len), BF16), pltpu.VMEM((rows, width, src_len), BF16)),
            in_specs=[HBM] * 12,
            out_specs=(VM,) * 6,
            scratch_shapes=[
                pltpu.VMEM((n, rows, width), BF16), pltpu.VMEM((1, width), F32), pltpu.VMEM((3, share, width), BF16),
                pltpu.VMEM((n * rows, 384), BF16), pltpu.VMEM((n, rows, 384), BF16),
                dma((9,)), dma((4,)), dma((7,)), dma((n,)), dma((7,)), dma((n,)), dma((14,)), dma((n, 2)),
            ],
            compiler_params=pltpu.CompilerParams(collective_id=0, has_side_effects=True,
                                                 vmem_limit_bytes=6 * 2 ** 20),
            name='proj_part',
        )(hidden, ln_self.reshape(1, width), wq_self.T, wk_self.T, wv_self.T, wo_self.T, wq_cross.T, wo_cross.T,
          flat(self_k), flat(self_v), flat(cross_k), flat(cross_v))

        newk, newv, ctx, win_v, wout_v = pl.pallas_call(
            functools.partial(self_kernel, head_dim),
            out_shape=(pltpu.HBM((rows, width, length), BF16), pltpu.HBM((rows, width, length), BF16),
                       pltpu.VMEM((rows, width), BF16), pltpu.VMEM(w_in.shape, BF16), pltpu.VMEM(w_out.shape, BF16)),
            in_specs=[SM, VM, VM, VM, VM, HBM, HBM],
            out_specs=(HBM, HBM, VM, VM, VM),
            scratch_shapes=[
                pltpu.VMEM((width, 128), F32), pltpu.VMEM((width, 128), F32), pltpu.VMEM((rows, width, 128), BF16),
                pltpu.VMEM((rows, width, 128), BF16), pltpu.VMEM((rows, heads_pad, length), F32),
                pltpu.VMEM((rows, heads_pad, length), BF16), pltpu.VMEM((rows, width), F32),
                pltpu.VMEM((heads_pad, length), F32),
                dma((2,)), dma((rows, length // 128)), dma((rows, length // 128)),
            ],
            compiler_params=pltpu.CompilerParams(has_side_effects=True, vmem_limit_bytes=12 * 2 ** 20),
            name='self_part',
        )(positions, qkv, rel_bias, kv_k, kv_v, w_in, w_out)

        out = pl.pallas_call(
            functools.partial(cross_kernel, n, head_dim, capacity),
            out_shape=jax.ShapeDtypeStruct((rows, width), BF16),
            in_specs=[SM, VM, VM] + [ANY] * 5 + [VM] * 4,
            out_specs=VM,
            scratch_shapes=[
                pltpu.VMEM((rows, width), BF16), pltpu.VMEM((1, width), F32), pltpu.VMEM((1, width), F32),
                pltpu.VMEM((rows, src_len), jnp.int32), pltpu.VMEM((n, 1, width), F32),
                pltpu.VMEM((n, rows, 128), jnp.int32), pltpu.VMEM((rows, width), F32),
                pltpu.VMEM((rows, heads_pad, src_len), F32), pltpu.VMEM((rows, heads_pad, src_len), BF16),
                pltpu.VMEM((rows, width), F32), pltpu.VMEM((n, rows, width), BF16),
                pltpu.VMEM((experts, n * rows, units), BF16), pltpu.VMEM((width // chunk, n * rows, chunk), F32),
                pltpu.VMEM((n, width // chunk, rows, chunk), F32),
                dma((5,)), dma((7,)), dma((n,)), dma((7,)), dma((n,)), dma((7,)),
                dma((n,)), dma((width // chunk, 7)), dma((width // chunk, n)),
            ],
            compiler_params=pltpu.CompilerParams(collective_id=1, has_side_effects=True,
                                                 vmem_limit_bytes=14 * 2 ** 20),
            name='cross_part',
        )(expert_idx, ctx, wall, hidden, ln_cross.reshape(1, width), ln_ffn.reshape(1, width), enc_mask, w_router.T,
          c_k, c_v, win_v, wout_v)

        def unflat(cache):
            return jnp.swapaxes(cache.reshape(rows, heads, head_dim, length), 2, 3)
        return out, unflat(newk), unflat(newv)

    return jax.shard_map(decoder_block, mesh=mesh, in_specs=in_specs, out_specs=out_specs, check_vma=False)
```

time: 594 us -> 90.9 us (0.15)
  waiting for transfers between devices: 285 us -> 0 us
  local copies, waits for them, and re-layouts: 168 us -> 33.2 us
  matrix products: 80.6 us -> 0 us
  Pallas kernels: 0 us -> 56.3 us
  blocking collectives: 23.8 us -> 0 us
  other arithmetic: 20.1 us -> 0 us
  between operations: 15.2 us -> 0.79 us
    all_gather x8 -> x0, waiting for transfers between devices: 280 us -> none  [the longest x1 171 us: decoder_block(): win_full = gather_ws(w_in, axis=2)]
    gather x9 -> x0, local copies, waits for them, and re-layouts: 158 us -> none  [the longest x4 69.2 us: decoder_block(): jnp.take(wout_full, expert_idx, axis=0)]
    dot_general x13 -> x0, matrix products: 80.6 us -> none  [the longest x1 27.4 us: decoder_block(): jnp.einsum('bd,bdf->bf', x_norm, jnp.take(win_full, expert_idx, axis=0),...]
    pallas_call x0 -> x3, Pallas kernels: none -> 56.3 us  [the longest x1 26.1 us: decoder_block(): pl.pallas_call(functools.partial(proj_kernel, n), out_shape=(pltpu.VMEM((...]
    unnamed x30 -> x51, local copies, waits for them, and re-layouts: 5.49 us -> 32.5 us
    all_gather x1 -> x0, blocking collectives: 14.9 us -> none  [decoder_block(): router_full = gather_ws(w_router, axis=1)]
    select_n x5 -> x0, other arithmetic: 13.5 us -> none  [the longest x1 12.2 us: decoder_block(): new_self_v = jnp.where(write_mask, v_new[:, :, None, :], self_v)]
    unnamed x1 -> x0, blocking collectives: 8.95 us -> none
  transfers between devices with their start and end apart: 8 -> 0, of which waited for: 5 -> 0; matrix products, arithmetic and copies ran while one was open for 29% -> 0% of each run, Pallas kernels for 0% -> 0%
where the time goes in v1:
time: 90.9 us; the launch traced here: 90.3 us
  Pallas kernels  56.3 us (62%)
  local copies, waits for them, and re-layouts  33.2 us (37%)
    unnamed x51, local copies, waits for them, and re-layouts  32.5 us
    pallas_call x1, Pallas kernels, decoder_block(): pl.pallas_call(functools.partial(proj_kernel, n), out_shape=(pltpu.VMEM((...  26.1 us
    pallas_call x1, Pallas kernels, decoder_block(): pl.pallas_call(functools.partial(cross_kernel, n, head_dim, capacity), ou...  21.1 us
    pallas_call x1, Pallas kernels, decoder_block(): pl.pallas_call(functools.partial(self_kernel, head_dim), out_shape=(pltpu...  9.05 us

profile of v1, /device:TPU:81, one launch (start us, length us, event | category | flops | bytes accessed | tf_op | source)
XLA Modules:
  0.0 90.3 jit_solution(7942093522817602592)
XLA Ops:
  0.6 0.7 reshape.33.ln_hbm
  1.3 0.0 copy-start.2
  1.3 2.8 %copy-done.2 = bf16[16,12,192,64]{2,3,1,0:T(8,128)(2,1)S(1)} copy-done((bf16[16,12,192,64]{2,3,1,0:T(8,128)(2,1)S(1)}, bf16[16,12,192,64]{2,3,1,0:T(8,128)(2,1)}, u32[]{:S(2)}) %copy-start.2) | copy-done | bytes 4718616
  4.1 0.0 copy-start.3
  4.1 2.8 %copy-done.3 = bf16[16,12,192,64]{2,3,1,0:T(8,128)(2,1)S(1)} copy-done((bf16[16,12,192,64]{2,3,1,0:T(8,128)(2,1)S(1)}, bf16[16,12,192,64]{2,3,1,0:T(8,128)(2,1)}, u32[]{:S(2)}) %copy-start.3) | copy-done | bytes 4718616
  6.9 0.0 copy-start.10
  6.9 0.9 %copy-done.10 = bf16[768,96]{0,1:T(8,128)(2,1)S(1)} copy-done((bf16[768,96]{0,1:T(8,128)(2,1)S(1)}, bf16[768,96]{0,1:T(8,128)(2,1)}, u32[]{:S(2)}) %copy-start.10) | copy-done | bytes 147480
  7.8 0.0 copy-start.11
  7.8 0.9 %copy-done.11 = bf16[768,96]{0,1:T(8,128)(2,1)S(1)} copy-done((bf16[768,96]{0,1:T(8,128)(2,1)S(1)}, bf16[768,96]{0,1:T(8,128)(2,1)}, u32[]{:S(2)}) %copy-start.11) | copy-done | bytes 147480
  8.7 0.0 copy-start.12
  8.7 0.9 %copy-done.12 = bf16[768,96]{0,1:T(8,128)(2,1)S(1)} copy-done((bf16[768,96]{0,1:T(8,128)(2,1)S(1)}, bf16[768,96]{0,1:T(8,128)(2,1)}, u32[]{:S(2)}) %copy-start.12) | copy-done | bytes 147480
  9.6 0.0 copy-start.13
  9.6 0.9 %copy-done.13 = bf16[768,96]{0,1:T(8,128)(2,1)S(1)} copy-done((bf16[768,96]{0,1:T(8,128)(2,1)S(1)}, bf16[768,96]{0,1:T(8,128)(2,1)}, u32[]{:S(2)}) %copy-start.13) | copy-done | bytes 147480
  10.5 0.0 copy-start.14
  10.5 0.9 %copy-done.14 = bf16[768,96]{0,1:T(8,128)(2,1)S(1)} copy-done((bf16[768,96]{0,1:T(8,128)(2,1)S(1)}, bf16[768,96]{0,1:T(8,128)(2,1)}, u32[]{:S(2)}) %copy-start.14) | copy-done | bytes 147480
  11.4 0.0 copy-start.15
  11.4 0.9 %copy-done.15 = bf16[768,96]{0,1:T(8,128)(2,1)S(1)} copy-done((bf16[768,96]{0,1:T(8,128)(2,1)S(1)}, bf16[768,96]{0,1:T(8,128)(2,1)}, u32[]{:S(2)}) %copy-start.15) | copy-done | bytes 147480
  12.4 0.0 copy-start.16
  12.4 0.7 copy-done.16
  13.1 0.0 copy-start.18
  13.1 0.0 copy-start.22
  13.1 26.1 %proj_part.1 = (f32[3,16,768]{2,1,0:T(8,128)S(1)}, bf16[8,288,768]{2,1,0:T(8,128)(2,1)S(1)}, bf16[16,768,384]{2,1,0:T(8,128)(2,1)S(1)}, bf16[16,768,384]{2,1,0:T...) custom-call(bf16[16,768]{1,0:T(8,128)(2,1)S(1)} %copy-done.16, ...), custom_call_target="tpu_custom_call" | custom-call | tf_op jit(solution)/shard_map/proj_part/pallas_call | solution.py:417
  39.2 0.0 copy-start
  39.2 3.7 %copy-done = bf16[16,768,384]{2,1,0:T(8,128)(2,1)} copy-done((bf16[16,768,384]{2,1,0:T(8,128)(2,1)}, bf16[16,768,384]{2,1,0:T(8,128)(2,1)S(1)}, u32[]{:S(2)}) %copy-start) | copy-done | bytes 9437208
  43.0 0.0 copy-start.4
  43.0 2.7 %copy-done.4 = bf16[16,768,192]{2,1,0:T(8,128)(2,1)} copy-done((bf16[16,768,192]{2,1,0:T(8,128)(2,1)}, bf16[16,768,192]{2,1,0:T(8,128)(2,1)S(1)}, u32[]{:S(2)}) %copy-start.4) | copy-done | bytes 4718616
  45.6 0.0 copy-start.6
  45.6 2.6 %copy-done.6 = bf16[16,768,192]{2,1,0:T(8,128)(2,1)} copy-done((bf16[16,768,192]{2,1,0:T(8,128)(2,1)}, bf16[16,768,192]{2,1,0:T(8,128)(2,1)S(1)}, u32[]{:S(2)}) %copy-start.6) | copy-done | bytes 4718616
  48.2 0.0 copy-done.18
  48.2 0.0 copy-done.22
  48.2 0.0 copy-start.1
  48.2 3.7 %copy-done.1 = bf16[16,768,384]{2,1,0:T(8,128)(2,1)S(1)} copy-done((bf16[16,768,384]{2,1,0:T(8,128)(2,1)S(1)}, bf16[16,768,384]{2,1,0:T(8,128)(2,1)}, u32[]{:S(2)}) %copy-start.1) | copy-done | bytes 9437208
  51.9 0.0 copy-start.8
  51.9 2.3 %copy-done.8 = bf16[8,768,384]{2,1,0:T(8,128)(2,1)S(1)} copy-done((bf16[8,768,384]{2,1,0:T(8,128)(2,1)S(1)}, bf16[8,768,384]{2,1,0:T(8,128)(2,1)}, u32[]{:S(2)}) %copy-start.8) | copy-done | bytes 4718616
  54.2 0.0 copy-start.9
  54.3 2.3 %copy-done.9 = bf16[8,384,768]{2,1,0:T(8,128)(2,1)S(1)} copy-done((bf16[8,384,768]{2,1,0:T(8,128)(2,1)S(1)}, bf16[8,384,768]{2,1,0:T(8,128)(2,1)}, u32[]{:S(2)}) %copy-start.9) | copy-done | bytes 4718616
  56.6 0.0 copy-start.23
  56.6 0.0 copy-start.24
  56.6 0.0 copy-start.7
  56.6 0.0 copy-start.17
  56.6 0.0 copy-start.19
  56.6 0.0 copy-start.20
  56.6 0.0 copy-start.21
  56.6 9.0 %self_part.1 = (bf16[16,768,384]{2,1,0:T(8,128)(2,1)}, bf16[16,768,384]{2,1,0:T(8,128)(2,1)}, bf16[16,768]{1,0:T(8,128)(2,1)S(1)}, bf16[8,768,384]{2,1,0:T(8,128)(2,1)S(1)}, bf16[8,384,768]{2,1,0:T(8,128)(2,1)S(1)}) custom-call(s32[16]{0:T(128)S(1)} %copy-done.22, f32[3,16,768]{2,1,0:T(8,128)S(1)} %get-tuple-element.14.qkv_ref, f32[12,384]{1,0:T(8,128)S(1)} %copy-done.18, ...), custom_call_target="tpu_custom_call" | custom-call | tf_op jit(solution)/shard_map/self_part/pallas_call | solution.py:435
  65.7 0.0 copy-done.23
  65.7 0.0 copy-done.24
  65.7 0.0 copy-done.7
  65.7 0.0 copy-done.17
  65.8 0.0 copy-done.19
  65.8 0.0 copy-done.20
  65.8 0.0 copy-done.21
  65.8 0.0 copy-start.5
  65.8 2.8 %copy-done.5 = bf16[16,768,192]{2,1,0:T(8,128)(2,1)S(1)} copy-done((bf16[16,768,192]{2,1,0:T(8,128)(2,1)S(1)}, bf16[16,768,192]{2,1,0:T(8,128)(2,1)}, u32[]{:S(2)}) %copy-start.5) | copy-done | bytes 4718616
  68.6 21.1 %cross_part.1 = bf16[16,768]{1,0:T(8,128)(2,1)S(1)} custom-call(s32[16]{0:T(128)S(1)} %copy-done.21, bf16[16,768]{1,0:T(8,128)(2,1)S(1)} %get-tuple-element.17.ctx_ref, bf16[8,288,768]{2,1,0:T(8,128)(2,1)S(1)} %get-tuple-element.18.wall_ref, bf16[16,768]{1,0:T(8,128)(2,1)S(1)} %copy-done.17, f32[1,768]{1,0:T(1,128)S(1)} %reshape.38.lnc_hbm, ...), custom_call_target="tpu_custom_call" | custom-call | tf_op jit(solution)/shard_map/cross_part/pallas_call | solution.py:452
  89.7 0.6 copy.25
  (2 shorter events, 0.0 us)
Async XLA Ops:
  1.3 2.8 %copy-start.2 = (bf16[16,12,192,64]{2,3,1,0:T(8,128)(2,1)S(1)}, bf16[16,12,192,64]{2,3,1,0:T(8,128)(2,1)}, u32[]{:S(2)}) copy-start(bf16[16,12,192,64]{2,3,1,0:T(8,128)(2,1)} %param.24) | copy-start | bytes 14155780
  4.1 2.8 %copy-start.3 = (bf16[16,12,192,64]{2,3,1,0:T(8,128)(2,1)S(1)}, bf16[16,12,192,64]{2,3,1,0:T(8,128)(2,1)}, u32[]{:S(2)}) copy-start(bf16[16,12,192,64]{2,3,1,0:T(8,128)(2,1)} %param.25) | copy-start | bytes 14155780
  6.9 0.9 %copy-start.10 = (bf16[768,96]{0,1:T(8,128)(2,1)S(1)}, bf16[768,96]{0,1:T(8,128)(2,1)}, u32[]{:S(2)}) copy-start(bf16[768,96]{0,1:T(8,128)(2,1)} %param.33) | copy-start | bytes 442372
  7.8 0.9 %copy-start.11 = (bf16[768,96]{0,1:T(8,128)(2,1)S(1)}, bf16[768,96]{0,1:T(8,128)(2,1)}, u32[]{:S(2)}) copy-start(bf16[768,96]{0,1:T(8,128)(2,1)} %param.34) | copy-start | bytes 442372
  8.7 0.9 %copy-start.12 = (bf16[768,96]{0,1:T(8,128)(2,1)S(1)}, bf16[768,96]{0,1:T(8,128)(2,1)}, u32[]{:S(2)}) copy-start(bf16[768,96]{0,1:T(8,128)(2,1)} %param.35) | copy-start | bytes 442372
  9.6 0.9 %copy-start.13 = (bf16[768,96]{0,1:T(8,128)(2,1)S(1)}, bf16[768,96]{0,1:T(8,128)(2,1)}, u32[]{:S(2)}) copy-start(bf16[768,96]{0,1:T(8,128)(2,1)} %param.36) | copy-start | bytes 442372
  10.5 0.9 %copy-start.14 = (bf16[768,96]{0,1:T(8,128)(2,1)S(1)}, bf16[768,96]{0,1:T(8,128)(2,1)}, u32[]{:S(2)}) copy-start(bf16[768,96]{0,1:T(8,128)(2,1)} %param.37) | copy-start | bytes 442372
  11.4 0.9 %copy-start.15 = (bf16[768,96]{0,1:T(8,128)(2,1)S(1)}, bf16[768,96]{0,1:T(8,128)(2,1)}, u32[]{:S(2)}) copy-start(bf16[768,96]{0,1:T(8,128)(2,1)} %param.38) | copy-start | bytes 442372
  12.4 0.7 copy-start.16
  13.1 35.1 %copy-start.18 = (f32[12,384]{1,0:T(8,128)S(1)}, f32[12,384]{1,0:T(8,128)}, u32[]{:S(2)}) copy-start(f32[12,384]{1,0:T(8,128)} %rel_ref.1) | copy-start | bytes 55300
  13.1 35.1 %copy-start.22 = (s32[16]{0:T(128)S(1)}, s32[16]{0:T(128)}, u32[]{:S(2)}) copy-start(s32[16]{0:T(128)} %pos_ref.1) | copy-start | bytes 196
  39.2 3.7 %copy-start = (bf16[16,768,384]{2,1,0:T(8,128)(2,1)}, bf16[16,768,384]{2,1,0:T(8,128)(2,1)S(1)}, u32[]{:S(2)}) copy-start(bf16[16,768,384]{2,1,0:T(8,128)(2,1)S(1)} %get-tuple-element.16.v_ref) | copy-start | bytes 28311556
  43.0 2.7 %copy-start.4 = (bf16[16,768,192]{2,1,0:T(8,128)(2,1)}, bf16[16,768,192]{2,1,0:T(8,128)(2,1)S(1)}, u32[]{:S(2)}) copy-start(bf16[16,768,192]{2,1,0:T(8,128)(2,1)S(1)} %get-tuple-element.19.k_ref) | copy-start | bytes 14155780
  45.6 2.6 %copy-start.6 = (bf16[16,768,192]{2,1,0:T(8,128)(2,1)}, bf16[16,768,192]{2,1,0:T(8,128)(2,1)S(1)}, u32[]{:S(2)}) copy-start(bf16[16,768,192]{2,1,0:T(8,128)(2,1)S(1)} %get-tuple-element.20.v_ref) | copy-start | bytes 14155780
  48.2 3.7 %copy-start.1 = (bf16[16,768,384]{2,1,0:T(8,128)(2,1)S(1)}, bf16[16,768,384]{2,1,0:T(8,128)(2,1)}, u32[]{:S(2)}) copy-start(bf16[16,768,384]{2,1,0:T(8,128)(2,1)} %copy-done) | copy-start | bytes 28311556
  51.9 2.3 %copy-start.8 = (bf16[8,768,384]{2,1,0:T(8,128)(2,1)S(1)}, bf16[8,768,384]{2,1,0:T(8,128)(2,1)}, u32[]{:S(2)}) copy-start(bf16[8,768,384]{2,1,0:T(8,128)(2,1)} %win_hbm.1) | copy-start | bytes 14155780
  54.2 2.3 %copy-start.9 = (bf16[8,384,768]{2,1,0:T(8,128)(2,1)S(1)}, bf16[8,384,768]{2,1,0:T(8,128)(2,1)}, u32[]{:S(2)}) copy-start(bf16[8,384,768]{2,1,0:T(8,128)(2,1)} %wout_hbm.1) | copy-start | bytes 14155780
  56.6 9.1 %copy-start.23 = (f32[768]{0:T(1024)S(1)}, f32[768]{0:T(1024)}, u32[]{:S(2)}) copy-start(f32[768]{0:T(1024)} %param.31) | copy-start | bytes 9220
  56.6 9.1 %copy-start.24 = (f32[768]{0:T(1024)S(1)}, f32[768]{0:T(1024)}, u32[]{:S(2)}) copy-start(f32[768]{0:T(1024)} %param.32) | copy-start | bytes 9220
  56.6 9.1 %copy-start.7 = (bf16[16,768,192]{2,1,0:T(8,128)(2,1)S(1)}, bf16[16,768,192]{2,1,0:T(8,128)(2,1)}, u32[]{:S(2)}) copy-start(bf16[16,768,192]{2,1,0:T(8,128)(2,1)} %copy-done.6) | copy-start | bytes 14155780
  56.6 9.2 %copy-start.17 = (bf16[16,768]{1,0:T(8,128)(2,1)S(1)}, bf16[16,768]{1,0:T(8,128)(2,1)}, u32[]{:S(2)}) copy-start(bf16[16,768]{1,0:T(8,128)(2,1)} %hid_hbm.3) | copy-start | bytes 73732
  56.6 9.2 %copy-start.19 = (s32[16,192]{1,0:T(8,128)S(1)}, s32[16,192]{1,0:T(8,128)}, u32[]{:S(2)}) copy-start(s32[16,192]{1,0:T(8,128)} %mask_hbm.1) | copy-start | bytes 36868
  56.6 9.2 %copy-start.20 = (f32[768,1]{0,1:T(1,128)S(1)}, f32[768,1]{0,1:T(1,128)}, u32[]{:S(2)}) copy-start(f32[768,1]{0,1:T(1,128)} %param.39) | copy-start | bytes 9220
  56.6 9.2 %copy-start.21 = (s32[16]{0:T(128)S(1)}, s32[16]{0:T(128)}, u32[]{:S(2)}) copy-start(s32[16]{0:T(128)} %eidx_ref.1) | copy-start | bytes 196
  65.8 2.8 %copy-start.5 = (bf16[16,768,192]{2,1,0:T(8,128)(2,1)S(1)}, bf16[16,768,192]{2,1,0:T(8,128)(2,1)}, u32[]{:S(2)}) copy-start(bf16[16,768,192]{2,1,0:T(8,128)(2,1)} %copy-done.4) | copy-start | bytes 14155780

commit v2 on v1

--- a/solution.py
+++ b/solution.py
@@ -10,13 +10,20 @@
 NEG_BIG = -1e30
 F32, BF16 = jnp.float32, jnp.bfloat16
 MESH = pl.DeviceIdType.MESH
-ANY = pl.BlockSpec(memory_space=pl.ANY)
 VM = pl.BlockSpec(memory_space=pltpu.VMEM)
 HBM = pl.BlockSpec(memory_space=pltpu.HBM)
 SM = pl.BlockSpec(memory_space=pltpu.SMEM)
 NT = (((1,), (1,)), ((), ()))
 PEERS = ((2, 0), (2, 1), (1, 0), (3, 0), (1, 1), (3, 1), (0, 1))
 UNROLL = 4
+
+
+def in_hbm(*arrays):
+    return [pltpu.with_memory_space_constraint(a, pltpu.HBM) for a in arrays]
+
+
+def in_vmem(*arrays):
+    return [pltpu.with_memory_space_constraint(a, pltpu.VMEM) for a in arrays]
 
 
 def rms_norm(hid_f32, scale):
@@ -116,7 +123,7 @@
     for peer in PEERS:
         src = dev(*peer)
         remote(xall_ref.at[src], xall_ref.at[src], x_send.at[0], x_recv.at[src], src).wait_recv()
-    x_norm = rms_norm(xall_ref[...].reshape(n * rows, width).astype(F32), ln_ref[...])
+    x_norm = rms_norm(xall_ref[...].reshape(n * rows, width).astype(F32), ln_ref[...][None])
     for part in range(3):
         qsend_ref[:, part * 128:part * 128 + share] = dot_nt(x_norm, wqkv_ref[part]).astype(BF16)
     q_out = []
@@ -163,15 +170,21 @@
         copy.wait_send()
 
 
-def self_kernel(head_dim, pos_ref, qkv_ref, rel_ref, k_ref, v_ref, win_hbm, wout_hbm,
+def self_kernel(head_dim, pos_ref, qkv_ref, rel_hbm, k_ref, v_ref, win_hbm, wout_hbm,
                 newk_hbm, newv_hbm, ctx_ref, win_ref, wout_ref,
-                kt_ref, vt_ref, kp_ref, vp_ref, s_ref, p_ref, ctx32_ref, rrev_ref, w_sem, k_sem, v_sem):
+                kt_ref, vt_ref, kp_ref, vp_ref, s_ref, p_ref, ctx32_ref, rrev_ref, rel_ref, w_sem, k_sem, v_sem):
     rows, width, length = k_ref.shape
     heads_pad = s_ref.shape[1]
     steps = rows // UNROLL
     tiles = length // 128
     w_loads = [pltpu.make_async_copy(win_hbm, win_ref, w_sem.at[0]),
                pltpu.make_async_copy(wout_hbm, wout_ref, w_sem.at[1])]
+    rel_load = pltpu.make_async_copy(rel_hbm, rel_ref, w_sem.at[2])
+    rel_load.start()
+    pad = jnp.zeros((128 - rows, width), F32)
+    kt_ref[...] = jnp.concatenate([qkv_ref[1], pad], axis=0).T
+    vt_ref[...] = jnp.concatenate([qkv_ref[2], pad], axis=0).T
+    rel_load.wait()
 
     rel = jnp.concatenate([rel_ref[...], jnp.zeros((heads_pad - rel_ref.shape[0], length), F32)], axis=0)
     flip = (lax.broadcasted_iota(jnp.int32, (length, length), 0) + lax.broadcasted_iota(jnp.int32, (length, length), 1)
@@ -182,9 +195,6 @@
     low = (rest - mid.astype(F32)).astype(BF16)
     rrev_ref[...] = (jnp.dot(hi, flip, preferred_element_type=F32) + jnp.dot(mid, flip, preferred_element_type=F32)
                      + jnp.dot(low, flip, preferred_element_type=F32))
-    pad = jnp.zeros((128 - rows, width), F32)
-    kt_ref[...] = jnp.concatenate([qkv_ref[1], pad], axis=0).T
-    vt_ref[...] = jnp.concatenate([qkv_ref[2], pad], axis=0).T
 
     h_mask = head_mask(heads_pad, width, head_dim)
     lane = lax.broadcasted_iota(jnp.int32, (1, length), 1)
@@ -285,7 +295,7 @@
     h1 = (hid_ref[...].astype(F32) + dot_nt(ctx_ref[...], wo)).astype(BF16).astype(F32)
     loads[1].wait()
     wqc = wall_ref[:, piece:piece + share, :].reshape(width, width)
-    q_ref[...] = dot_nt(rms_norm(h1, lnc_ref[...]), wqc).astype(BF16).astype(F32)
+    q_ref[...] = dot_nt(rms_norm(h1, lnc_ref[...][None]), wqc).astype(BF16).astype(F32)
 
     loads[4].wait()
     pl.semaphore_wait(barrier, n - 1)
@@ -322,7 +332,7 @@
     woc = woc.reshape(width, width)
     h2 = (h1 + dot_nt(ctx32_ref[...].astype(BF16), woc)).astype(BF16).astype(F32)
     loads[2].wait()
-    x_own = rms_norm(h2, lnf_ref[...])
+    x_own = rms_norm(h2, lnf_ref[...][None])
     xall_ref[me] = x_own
     x_out = [remote(xall_ref.at[me], xall_ref.at[me], x_send.at[i], x_recv.at[me], dev(*peer))
              for i, peer in enumerate(PEERS)]
@@ -422,40 +432,40 @@
             in_specs=[HBM] * 12,
             out_specs=(VM,) * 6,
             scratch_shapes=[
-                pltpu.VMEM((n, rows, width), BF16), pltpu.VMEM((1, width), F32), pltpu.VMEM((3, share, width), BF16),
+                pltpu.VMEM((n, rows, width), BF16), pltpu.VMEM((width,), F32), pltpu.VMEM((3, share, width), BF16),
                 pltpu.VMEM((n * rows, 384), BF16), pltpu.VMEM((n, rows, 384), BF16),
                 dma((9,)), dma((4,)), dma((7,)), dma((n,)), dma((7,)), dma((n,)), dma((14,)), dma((n, 2)),
             ],
             compiler_params=pltpu.CompilerParams(collective_id=0, has_side_effects=True,
                                                  vmem_limit_bytes=6 * 2 ** 20),
             name='proj_part',
-        )(hidden, ln_self.reshape(1, width), wq_self.T, wk_self.T, wv_self.T, wo_self.T, wq_cross.T, wo_cross.T,
-          flat(self_k), flat(self_v), flat(cross_k), flat(cross_v))
+        )(*in_hbm(hidden, ln_self, wq_self.T, wk_self.T, wv_self.T, wo_self.T, wq_cross.T, wo_cross.T,
+                  flat(self_k), flat(self_v), flat(cross_k), flat(cross_v)))
 
         newk, newv, ctx, win_v, wout_v = pl.pallas_call(
             functools.partial(self_kernel, head_dim),
             out_shape=(pltpu.HBM((rows, width, length), BF16), pltpu.HBM((rows, width, length), BF16),
                        pltpu.VMEM((rows, width), BF16), pltpu.VMEM(w_in.shape, BF16), pltpu.VMEM(w_out.shape, BF16)),
-            in_specs=[SM, VM, VM, VM, VM, HBM, HBM],
+            in_specs=[SM, VM, HBM, VM, VM, HBM, HBM],
             out_specs=(HBM, HBM, VM, VM, VM),
             scratch_shapes=[
                 pltpu.VMEM((width, 128), F32), pltpu.VMEM((width, 128), F32), pltpu.VMEM((rows, width, 128), BF16),
                 pltpu.VMEM((rows, width, 128), BF16), pltpu.VMEM((rows, heads_pad, length), F32),
                 pltpu.VMEM((rows, heads_pad, length), BF16), pltpu.VMEM((rows, width), F32),
-                pltpu.VMEM((heads_pad, length), F32),
-                dma((2,)), dma((rows, length // 128)), dma((rows, length // 128)),
+                pltpu.VMEM((heads_pad, length), F32), pltpu.VMEM((heads, length), F32),
+                dma((3,)), dma((rows, length // 128)), dma((rows, length // 128)),
             ],
             compiler_params=pltpu.CompilerParams(has_side_effects=True, vmem_limit_bytes=12 * 2 ** 20),
             name='self_part',
-        )(positions, qkv, rel_bias, kv_k, kv_v, w_in, w_out)
+        )(positions, *in_vmem(qkv), *in_hbm(rel_bias), *in_vmem(kv_k, kv_v), *in_hbm(w_in, w_out))
 
         out = pl.pallas_call(
             functools.partial(cross_kernel, n, head_dim, capacity),
             out_shape=jax.ShapeDtypeStruct((rows, width), BF16),
-            in_specs=[SM, VM, VM] + [ANY] * 5 + [VM] * 4,
+            in_specs=[SM, VM, VM] + [HBM] * 5 + [VM] * 4,
             out_specs=VM,
             scratch_shapes=[
-                pltpu.VMEM((rows, width), BF16), pltpu.VMEM((1, width), F32), pltpu.VMEM((1, width), F32),
+                pltpu.VMEM((rows, width), BF16), pltpu.VMEM((width,), F32), pltpu.VMEM((width,), F32),
                 pltpu.VMEM((rows, src_len), jnp.int32), pltpu.VMEM((n, 1, width), F32),
                 pltpu.VMEM((n, rows, 128), jnp.int32), pltpu.VMEM((rows, width), F32),
                 pltpu.VMEM((rows, heads_pad, src_len), F32), pltpu.VMEM((rows, heads_pad, src_len), BF16),
@@ -468,8 +478,8 @@
             compiler_params=pltpu.CompilerParams(collective_id=1, has_side_effects=True,
                                                  vmem_limit_bytes=14 * 2 ** 20),
             name='cross_part',
-        )(expert_idx, ctx, wall, hidden, ln_cross.reshape(1, width), ln_ffn.reshape(1, width), enc_mask, w_router.T,
-          c_k, c_v, win_v, wout_v)
+        )(expert_idx, *in_vmem(ctx, wall), *in_hbm(hidden, ln_cross, ln_ffn, enc_mask, w_router.T),
+          *in_vmem(c_k, c_v, win_v, wout_v))
 
         def unflat(cache):
             return jnp.swapaxes(cache.reshape(rows, heads, head_dim, length), 2, 3)

time: 90.9 us -> 61.8 us (0.68)
  local copies, waits for them, and re-layouts: 33.2 us -> 0.62 us
  Pallas kernels: 56.3 us -> 60.3 us
    unnamed x51 -> x5, local copies, waits for them, and re-layouts: 32.5 us -> 0.62 us
    pallas_call x1, Pallas kernels: 9.05 us -> 12.6 us  [decoder_block(): pl.pallas_call(functools.partial(self_kernel, head_dim), out_shape=(pltpu...]
where the time goes in v2:
time: 61.8 us; the launch traced here: 61.6 us
  Pallas kernels  60.3 us (98%)
  between operations  0.69 us (1%)
  local copies, waits for them, and re-layouts  0.62 us (1%)
    pallas_call x1, Pallas kernels, decoder_block(): pl.pallas_call(functools.partial(proj_kernel, n), out_shape=(pltpu.VMEM((...  26.1 us
    pallas_call x1, Pallas kernels, decoder_block(): pl.pallas_call(functools.partial(cross_kernel, n, head_dim, capacity), ou...  21.6 us
    pallas_call x1, Pallas kernels, decoder_block(): pl.pallas_call(functools.partial(self_kernel, head_dim), out_shape=(pltpu...  12.6 us

profile of v2, /device:TPU:81, one launch (start us, length us, event | category | flops | bytes accessed | tf_op | source)
XLA Modules:
  0.0 61.6 jit_solution(13509600242327781120)
XLA Ops:
  0.6 0.0 copy-start.1
  0.6 26.1 %proj_part.1 = (f32[3,16,768]{2,1,0:T(8,128)S(1)}, bf16[8,288,768]{2,1,0:T(8,128)(2,1)S(1)}, bf16[16,768,384]{2,1,0:T(8,128)(2,1)S(1)}, bf16[16,768,384]{2,1,0:T...) custom-call(bf16[16,768]{1,0:T(8,128)(2,1)} %hid_hbm.3, f32[768]{0:T(1024)} %ln_hbm.1, ...), custom_call_target="tpu_custom_call" | custom-call | tf_op jit(solution)/shard_map/proj_part/pallas_call | solution.py:427
  26.8 0.0 copy-done.1
  26.8 0.0 copy-start
  26.8 12.6 %self_part.1 = (bf16[16,768,384]{2,1,0:T(8,128)(2,1)}, bf16[16,768,384]{2,1,0:T(8,128)(2,1)}, bf16[16,768]{1,0:T(8,128)(2,1)S(1)}, bf16[8,768,384]{2,1,0:T(8,128)(2,1)S(1)}, bf16[8,384,768]{2,1,0:T(8,128)(2,1)S(1)}) custom-call(s32[16]{0:T(128)S(1)} %copy-done.1, f32[3,16,768]{2,1,0:T(8,128)S(1)} %get-tuple-element.14.qkv_ref, f32[12,384]{1,0:T(8,128)} %rel_hbm.1, ...), custom_call_target="tpu_custom_call" | custom-call | tf_op jit(solution)/shard_map/self_part/pallas_call | solution.py:445
  39.4 0.0 copy-done
  39.4 21.6 %cross_part.1 = bf16[16,768]{1,0:T(8,128)(2,1)S(1)} custom-call(s32[16]{0:T(128)S(1)} %copy-done, bf16[16,768]{1,0:T(8,128)(2,1)S(1)} %get-tuple-element.17.ctx_ref, bf16[8,288,768]{2,1,0:T(8,128)(2,1)S(1)} %get-tuple-element.18.wall_ref, bf16[16,768]{1,0:T(8,128)(2,1)} %hid_hbm.3, f32[768]{0:T(1024)} %lnc_hbm.1, f32[768]{0:T(1024)} %lnf_hbm.1, ...), custom_call_target="tpu_custom_call" | custom-call | tf_op jit(solution)/shard_map/cross_part/pallas_call | solution.py:462
  61.0 0.6 copy.25
Async XLA Ops:
  0.6 26.2 %copy-start.1 = (s32[16]{0:T(128)S(1)}, s32[16]{0:T(128)}, u32[]{:S(2)}) copy-start(s32[16]{0:T(128)} %pos_ref.1) | copy-start | bytes 196
  26.8 12.6 %copy-start = (s32[16]{0:T(128)S(1)}, s32[16]{0:T(128)}, u32[]{:S(2)}) copy-start(s32[16]{0:T(128)} %eidx_ref.1) | copy-start | bytes 196

commit v3 on v2

v3 whole, which is shorter than its diff:
```python
import functools
import jax
import jax.numpy as jnp
from jax import lax
from jax.experimental import pallas as pl
from jax.experimental.pallas import tpu as pltpu
from jax.sharding import PartitionSpec as P

EPSILON = 1e-6
NEG_BIG = -1e30
F32, BF16 = jnp.float32, jnp.bfloat16
MESH = pl.DeviceIdType.MESH
VM = pl.BlockSpec(memory_space=pltpu.VMEM)
HBM = pl.BlockSpec(memory_space=pltpu.HBM)
SM = pl.BlockSpec(memory_space=pltpu.SMEM)
NT = (((1,), (1,)), ((), ()))
PEERS = ((2, 0), (2, 1), (1, 0), (3, 0), (1, 1), (3, 1), (0, 1))
UNROLL = 4


def in_hbm(*arrays):
    return [pltpu.with_memory_space_constraint(a, pltpu.HBM) for a in arrays]


def in_vmem(*arrays):
    return [pltpu.with_memory_space_constraint(a, pltpu.VMEM) for a in arrays]


def rms_norm(hid_f32, scale):
    inv_rms = lax.rsqrt(jnp.mean(hid_f32 * hid_f32, axis=-1, keepdims=True) + EPSILON)
    return (hid_f32 * inv_rms * scale).astype(BF16)


def dot_nt(a, b):
    return lax.dot_general(a, b, NT, preferred_element_type=F32)


def softmax_rows(scores):
    top = jnp.max(scores, axis=-1, keepdims=True)
    ex = jnp.exp(scores - top)
    return (ex / jnp.sum(ex, axis=-1, keepdims=True)).astype(BF16)


def make_dev(n):
    me = lax.axis_index('ws')
    chips = n // 2
    chip, core = me // 2, lax.rem(me, 2)

    def dev(step, other):
        return 2 * lax.rem(chip + step, chips) + ((1 - core) if other else core)
    return me, dev


def remote(src, dst, send_sem, recv_sem, dev):
    return pltpu.make_async_remote_copy(src_ref=src, dst_ref=dst, send_sem=send_sem, recv_sem=recv_sem,
                                        device_id={'ws': dev}, device_id_type=MESH)


def head_mask(heads_pad, width, head_dim):
    row = lax.broadcasted_iota(jnp.int32, (heads_pad, width), 0)
    col = lax.broadcasted_iota(jnp.int32, (heads_pad, width), 1)
    return (col // head_dim == row).astype(F32)


def self_kernel(n, head_dim, pos_ref, eidx_ref, hid_hbm, ln_hbm, rel_hbm, wr_hbm, wq_hbm, wk_hbm, wv_hbm, wo_hbm,
                wqc_hbm, woc_hbm, k_hbm, v_hbm, ck_hbm, cv_hbm, win_hbm, wout_hbm,
                ctx_ref, kv_ref, wall_ref, wr_ref, eall_ref, k_ref, v_ref, ck_ref, cv_ref, win_ref, wout_ref,
                xall_ref, ln_ref, rel_ref, wqkv_ref, qsend_ref, qrecv_ref, q_ref, s_ref, p_ref, ctx32_ref, rrev_ref,
                in_sem, k_sem, v_sem, big_sem, x_send, x_recv, r_send, r_recv, e_send, e_recv, q_send, q_recv,
                w_send, w_recv):
    me, dev = make_dev(n)
    rows, width, length = k_ref.shape
    heads_pad = s_ref.shape[1]
    share = width // n
    half = share // 2
    steps = rows // UNROLL
    pieces = ((0, share), (share, share), (2 * share, half), (2 * share + half, half))

    barrier = pltpu.get_barrier_semaphore()
    for peer in PEERS:
        pl.semaphore_signal(barrier, inc=1, device_id={'ws': dev(*peer)}, device_id_type=MESH)

    mine = wall_ref.at[me]
    loads = [
        (hid_hbm, xall_ref.at[me]), (wr_hbm, wr_ref.at[me]), (ln_hbm, ln_ref), (wq_hbm, wqkv_ref.at[0]),
        (wk_hbm, wqkv_ref.at[1]), (wv_hbm, wqkv_ref.at[2]), (rel_hbm, rel_ref),
        (wo_hbm, mine.at[pl.ds(0, share)]), (wqc_hbm, mine.at[pl.ds(share, share)]),
        (woc_hbm, mine.at[pl.ds(2 * share, share)]),
    ]
    loads = [pltpu.make_async_copy(src, dst, in_sem.at[i]) for i, (src, dst) in enumerate(loads)]
    for load in loads:
        load.start()
    lane_id = lax.broadcasted_iota(jnp.int32, (1, 128), 1)
    e_row = jnp.zeros((1, 128), jnp.int32)
    for b in range(rows):
        e_row = jnp.where(lane_id == b, eidx_ref[b], e_row)
    eall_ref[me] = e_row

    loads[0].wait()
    pl.semaphore_wait(barrier, n - 1)
    x_out = [remote(xall_ref.at[me], xall_ref.at[me], x_send.at[i], x_recv.at[me], dev(*peer))
             for i, peer in enumerate(PEERS)]
    for copy in x_out:
        copy.start()
    for load in loads[7:]:
        load.wait()

    right, left, far, sib = dev(1, 0), dev(3, 0), dev(2, 0), dev(0, 1)
    w_out = []

    def send_piece(owner, part, target):
        start, size = pieces[part]
        block = wall_ref.at[owner, pl.ds(start, size)]
        copy = remote(block, block, w_send.at[len(w_out)], w_recv.at[owner, part], target)
        copy.start()
        w_out.append(copy)

    def wait_piece(owner, part):
        start, size = pieces[part]
        block = wall_ref.at[owner, pl.ds(start, size)]
        remote(block, block, w_send.at[0], w_recv.at[owner, part], sib).wait_recv()

    send_piece(me, 0, right)
    send_piece(me, 1, left)
    loads[1].wait()
    small = []
    for i, peer in enumerate(PEERS):
        dst = dev(*peer)
        small.append(remote(wr_ref.at[me], wr_ref.at[me], r_send.at[i], r_recv.at[me], dst))
        small.append(remote(eall_ref.at[me], eall_ref.at[me], e_send.at[i], e_recv.at[me], dst))
    k_loads = [pltpu.make_async_copy(k_hbm.at[pl.ds(i * UNROLL, UNROLL)], k_ref.at[pl.ds(i * UNROLL, UNROLL)],
                                     k_sem.at[i]) for i in range(steps)]
    v_loads = [pltpu.make_async_copy(v_hbm.at[pl.ds(i * UNROLL, UNROLL)], v_ref.at[pl.ds(i * UNROLL, UNROLL)],
                                     v_sem.at[i]) for i in range(steps)]
    big = [pltpu.make_async_copy(src, dst, big_sem.at[i]) for i, (src, dst) in
           enumerate([(ck_hbm, ck_ref), (cv_hbm, cv_ref), (win_hbm, win_ref), (wout_hbm, wout_ref)])]
    for load in k_loads + v_loads + big:
        load.start()

    loads[6].wait()
    rel = jnp.concatenate([rel_ref[...], jnp.zeros((heads_pad - rel_ref.shape[0], length), F32)], axis=0)
    flip = (lax.broadcasted_iota(jnp.int32, (length, length), 0) + lax.broadcasted_iota(jnp.int32, (length, length), 1)
            == length - 1).astype(F32).astype(BF16)
    hi = rel.astype(BF16)
    rest = rel - hi.astype(F32)
    mid = rest.astype(BF16)
    low = (rest - mid.astype(F32)).astype(BF16)
    rrev_ref[...] = (jnp.dot(hi, flip, preferred_element_type=F32) + jnp.dot(mid, flip, preferred_element_type=F32)
                     + jnp.dot(low, flip, preferred_element_type=F32))
    qsend_ref[...] = jnp.zeros_like(qsend_ref)

    for load in loads[2:6]:
        load.wait()
    for peer in PEERS:
        src = dev(*peer)
        remote(xall_ref.at[src], xall_ref.at[src], x_send.at[0], x_recv.at[src], src).wait_recv()
    x_norm = rms_norm(xall_ref[...].reshape(n * rows, width).astype(F32), ln_ref[...][None])
    for part in range(3):
        qsend_ref[:, part * 128:part * 128 + share] = dot_nt(x_norm, wqkv_ref[part]).astype(BF16)
    q_out = []
    for i, peer in enumerate(PEERS):
        dst = dev(*peer)
        q_out.append(remote(qsend_ref.at[pl.ds(dst * rows, rows)], qrecv_ref.at[me], q_send.at[i], q_recv.at[me], dst))
    for copy in q_out:
        copy.start()
    qrecv_ref[me] = qsend_ref[pl.ds(pl.multiple_of(me * rows, rows), rows), :]
    for target, order in ((right, (2, 1, 3)), (left, (3, 0, 2))):
        for part in order:
            send_piece(me, part, target)
    for part in range(len(pieces)):
        send_piece(me, part, sib)
    for copy in small:
        copy.start()

    for peer in PEERS:
        src = dev(*peer)
        remote(qrecv_ref.at[src], qrecv_ref.at[src], q_send.at[0], q_recv.at[src], src).wait_recv()
    wait_piece(left, 0)
    send_piece(left, 0, right)
    wait_piece(right, 1)
    send_piece(right, 1, left)
    send_piece(left, 0, sib)
    send_piece(right, 1, sib)

    def columns(part):
        return jnp.concatenate([qrecv_ref[s][:, part * 128:part * 128 + share] for s in range(n)], axis=1).astype(F32)
    q_ref[...] = columns(0)
    kv_ref[0] = columns(1)
    kv_ref[1] = columns(2)

    h_mask = head_mask(heads_pad, width, head_dim)
    lane = lax.broadcasted_iota(jnp.int32, (1, length), 1)

    def score_step(i, carry):
        pltpu.make_async_copy(k_hbm.at[pl.ds(i * UNROLL, UNROLL)], k_ref.at[pl.ds(i * UNROLL, UNROLL)],
                              k_sem.at[i]).wait()
        for s in range(UNROLL):
            b = i * UNROLL + s
            pos = pos_ref[b]
            q_diag = q_ref[pl.ds(b, 1), :] * h_mask
            scores = jnp.dot(q_diag.astype(BF16), k_ref[b], preferred_element_type=F32)
            new = jnp.sum(q_diag * kv_ref[0, pl.ds(b, 1), :], axis=1, keepdims=True)
            bias = pltpu.roll(rrev_ref[...], pos + 1, axis=1)
            s_ref[b] = jnp.where(lane <= pos, jnp.where(lane == pos, new, scores) + bias, NEG_BIG)
        return carry
    lax.fori_loop(0, steps, score_step, 0)

    wait_piece(left, 2)
    send_piece(left, 2, right)
    wait_piece(right, 3)
    send_piece(right, 3, left)
    send_piece(left, 2, sib)
    send_piece(right, 3, sib)

    p_ref[...] = softmax_rows(s_ref[...])

    def value_step(i, carry):
        pltpu.make_async_copy(v_hbm.at[pl.ds(i * UNROLL, UNROLL)], v_ref.at[pl.ds(i * UNROLL, UNROLL)],
                              v_sem.at[i]).wait()
        for s in range(UNROLL):
            b = i * UNROLL + s
            here = lane == pos_ref[b]
            probs = p_ref[b].astype(F32)
            new = jnp.sum(jnp.where(here, probs, 0.0), axis=1, keepdims=True)
            spread = dot_nt(jnp.where(here, 0.0, probs).astype(BF16), v_ref[b])
            spread = spread + new * kv_ref[1, pl.ds(b, 1), :]
            ctx32_ref[pl.ds(b, 1), :] = jnp.sum(spread * h_mask, axis=0, keepdims=True)
        return carry
    lax.fori_loop(0, steps, value_step, 0)
    ctx_ref[...] = ctx32_ref[...].astype(BF16)

    for owner, part in ((left, 1), (right, 0), (left, 3), (right, 2)):
        wait_piece(owner, part)
        send_piece(owner, part, sib)
    for part in range(len(pieces)):
        wait_piece(far, part)
        send_piece(far, part, sib)
    for step in range(n // 2):
        for part in range(len(pieces)):
            wait_piece(dev(step, 1), part)
    for peer in PEERS:
        src = dev(*peer)
        remote(wr_ref.at[src], wr_ref.at[src], r_send.at[0], r_recv.at[src], src).wait_recv()
        remote(eall_ref.at[src], eall_ref.at[src], e_send.at[0], e_recv.at[src], src).wait_recv()
    for load in big:
        load.wait()
    for copy in x_out + q_out + w_out + small:
        copy.wait_send()


def cross_kernel(head_dim, pos_ref, kv_ref, ctx_ref, wall_ref, hid_hbm, lnc_hbm, mask_hbm, k_ref, v_ref, ck_ref, cv_ref,
                 newk_hbm, newv_hbm, h1_ref, ctx2_ref,
                 hid_ref, lnc_ref, mask_ref, kt_ref, vt_ref, kp_ref, vp_ref, q_ref, s_ref, p_ref, ctx32_ref,
                 in_sem, k_sem, v_sem):
    rows, width, length = k_ref.shape
    heads_pad = s_ref.shape[1]
    share = width // wall_ref.shape[0]
    steps = rows // UNROLL
    tiles = length // 128
    loads = [(hid_hbm, hid_ref), (lnc_hbm, lnc_ref), (mask_hbm, mask_ref)]
    loads = [pltpu.make_async_copy(src, dst, in_sem.at[i]) for i, (src, dst) in enumerate(loads)]
    for load in loads:
        load.start()
    pad = jnp.zeros((128 - rows, width), F32)
    kt_ref[...] = jnp.concatenate([kv_ref[0], pad], axis=0).T
    vt_ref[...] = jnp.concatenate([kv_ref[1], pad], axis=0).T
    lane_tile = lax.broadcasted_iota(jnp.int32, (1, 128), 1)

    def out_copies(b, old_ref, patch_ref, new_hbm, sem):
        tile = pos_ref[b] // 128
        copies = []
        for k in range(tiles):
            cols = pl.ds(pl.multiple_of(lax.rem(tile + k, tiles) * 128, 128), 128)
            src = patch_ref.at[b] if k == 0 else old_ref.at[b, :, cols]
            copies.append(pltpu.make_async_copy(src, new_hbm.at[b, :, cols], sem.at[b, k]))
        return copies

    def put_row(b, column, old_ref, patch_ref, new_hbm, sem):
        pos = pos_ref[b]
        first = pl.multiple_of(pos // 128 * 128, 128)
        patch_ref[b] = jnp.where(lane_tile == pos - first, jnp.broadcast_to(column, (width, 128)).astype(BF16),
                                 old_ref[b, :, pl.ds(first, 128)])
        for copy in out_copies(b, old_ref, patch_ref, new_hbm, sem):
            copy.start()

    def patch_step(i, carry):
        kt = kt_ref[...]
        vt = vt_ref[...]
        for s in range(UNROLL):
            b = i * UNROLL + s
            put_row(b, kt[:, s:s + 1], k_ref, kp_ref, newk_hbm, k_sem)
            put_row(b, vt[:, s:s + 1], v_ref, vp_ref, newv_hbm, v_sem)
        kt_ref[...] = pltpu.roll(kt, 128 - UNROLL, axis=1)
        vt_ref[...] = pltpu.roll(vt, 128 - UNROLL, axis=1)
        return carry
    lax.fori_loop(0, steps, patch_step, 0)

    loads[0].wait()
    loads[1].wait()
    wo = wall_ref[:, 0:share, :].reshape(width, width)
    h1 = (hid_ref[...].astype(F32) + dot_nt(ctx_ref[...], wo)).astype(BF16).astype(F32)
    h1_ref[...] = h1
    wqc = wall_ref[:, share:2 * share, :].reshape(width, width)
    q_ref[...] = dot_nt(rms_norm(h1, lnc_ref[...][None]), wqc).astype(BF16).astype(F32)

    h_mask = head_mask(heads_pad, width, head_dim)
    loads[2].wait()

    def score_step(i, carry):
        for s in range(UNROLL):
            b = i * UNROLL + s
            q_diag = (q_ref[pl.ds(b, 1), :] * h_mask).astype(BF16)
            scores = jnp.dot(q_diag, ck_ref[b], preferred_element_type=F32)
            s_ref[b] = jnp.where(mask_ref[pl.ds(b, 1), :] == 1, scores, NEG_BIG)
        return carry
    lax.fori_loop(0, steps, score_step, 0)
    p_ref[...] = softmax_rows(s_ref[...])

    def value_step(i, carry):
        for s in range(UNROLL):
            b = i * UNROLL + s
            spread = dot_nt(p_ref[b], cv_ref[b])
            ctx32_ref[pl.ds(b, 1), :] = jnp.sum(spread * h_mask, axis=0, keepdims=True)
        return carry
    lax.fori_loop(0, steps, value_step, 0)
    ctx2_ref[...] = ctx32_ref[...].astype(BF16)

    def drain(b, carry):
        for copy in (out_copies(b, k_ref, kp_ref, newk_hbm, k_sem) + out_copies(b, v_ref, vp_ref, newv_hbm, v_sem)):
            copy.wait()
        return carry
    lax.fori_loop(0, rows, drain, 0)


def ffn_kernel(n, capacity, h1_ref, ctx2_ref, wall_ref, wr_ref, eall_ref, lnf_hbm, win_ref, wout_ref,
               out_ref,
               lnf_ref, xall_ref, u_ref, part_ref, rs_ref,
               in_sem, x_send, x_recv, rs_send, rs_recv):
    me, dev = make_dev(n)
    rows, width = h1_ref.shape
    share = width // n
    experts = win_ref.shape[0]
    barrier = pltpu.get_barrier_semaphore()
    for peer in PEERS:
        pl.semaphore_signal(barrier, inc=1, device_id={'ws': dev(*peer)}, device_id_type=MESH)
    load = pltpu.make_async_copy(lnf_hbm, lnf_ref, in_sem.at[0])
    load.start()
    woc = wall_ref[:, 2 * share:3 * share, :].reshape(width, width)
    h2 = (h1_ref[...] + dot_nt(ctx2_ref[...], woc)).astype(BF16).astype(F32)
    load.wait()
    x_own = rms_norm(h2, lnf_ref[...][None])
    xall_ref[me] = x_own
    pl.semaphore_wait(barrier, n - 1)
    x_out = [remote(xall_ref.at[me], xall_ref.at[me], x_send.at[i], x_recv.at[me], dev(*peer))
             for i, peer in enumerate(PEERS)]
    for copy in x_out:
        copy.start()

    x_f32 = x_own.astype(F32)
    logits = [jnp.sum(x_f32 * wr_ref[e], axis=-1, keepdims=True) for e in range(experts)]
    top = functools.reduce(jnp.maximum, logits)
    ex = [jnp.exp(v - top) for v in logits]
    total = functools.reduce(jnp.add, ex)
    e_pad = jnp.concatenate([eall_ref[...].reshape(n, 128), jnp.zeros((128 - n, 128), jnp.int32)], axis=0)
    e_cols = e_pad.astype(F32).T.astype(jnp.int32)
    e_all = jnp.concatenate([jnp.broadcast_to(e_cols[0:rows, s:s + 1], (rows, 128)) for s in range(n)], axis=0)
    row_id = lax.broadcasted_iota(jnp.int32, (rows, 128), 1)
    source = lax.broadcasted_iota(jnp.int32, (rows, 128), 1)
    e_own = jnp.sum(jnp.where(source == me, e_cols[0:rows, :], 0).astype(F32), axis=1, keepdims=True).astype(jnp.int32)
    gate = functools.reduce(jnp.add, [jnp.where(e_own == e, ex[e], 0.0) for e in range(experts)]) / total
    one_hot = (e_all == lax.broadcasted_iota(jnp.int32, (n * rows, 128), 1)).astype(F32).astype(BF16)
    earlier = (lax.broadcasted_iota(jnp.int32, (rows, n * rows), 1)
               < me * rows + lax.broadcasted_iota(jnp.int32, (rows, n * rows), 0)).astype(F32).astype(BF16)
    counts = jnp.dot(earlier, one_hot, preferred_element_type=F32)
    slot = jnp.sum(jnp.where(row_id == e_own, counts, 0.0), axis=-1, keepdims=True)
    keep_gate = jnp.where(slot < capacity, gate, 0.0)

    for peer in PEERS:
        src = dev(*peer)
        remote(xall_ref.at[src], xall_ref.at[src], x_send.at[0], x_recv.at[src], src).wait_recv()
    x_all = xall_ref[...].reshape(n * rows, width)
    e_wide = jnp.concatenate([e_all] * (win_ref.shape[2] // 128), axis=1)

    def expert_step(e, carry):
        u = jnp.maximum(jnp.dot(x_all, win_ref[e], preferred_element_type=F32), 0.0)
        u_ref[e] = jnp.where(e_wide == e, u, 0.0).astype(BF16)
        return carry
    lax.fori_loop(0, experts, expert_step, 0)

    chunk = part_ref.shape[2]
    rs_out = []
    for c in range(width // chunk):
        acc = jnp.zeros((n * rows, chunk), F32)
        for e in range(experts):
            acc = acc + jnp.dot(u_ref[e], wout_ref[e, :, c * chunk:(c + 1) * chunk], preferred_element_type=F32)
        part_ref[c] = acc
        rs_ref[me, c] = part_ref[c, pl.ds(pl.multiple_of(me * rows, rows), rows), :]
        for i, peer in enumerate(PEERS):
            dst = dev(*peer)
            copy = remote(part_ref.at[c, pl.ds(dst * rows, rows)], rs_ref.at[me, c], rs_send.at[c, i],
                          rs_recv.at[c, me], dst)
            copy.start()
            rs_out.append(copy)
    for c in range(width // chunk):
        for peer in PEERS:
            src = dev(*peer)
            remote(rs_ref.at[src, c], rs_ref.at[src, c], rs_send.at[c, 0], rs_recv.at[c, src], src).wait_recv()
        y = jnp.sum(rs_ref[:, c], axis=0).astype(BF16).astype(F32)
        cols = slice(c * chunk, (c + 1) * chunk)
        out_ref[:, cols] = (h2[:, cols] + y * keep_gate).astype(BF16)
    for copy in x_out + rs_out:
        copy.wait_send()


def solution(mesh):
    n = mesh.shape['ws']
    row_axes = ('dp', 'ws')
    row_vec = P(row_axes)
    row_mat = P(row_axes, None)
    cache_spec = P(row_axes, None, None, None)
    col_split = P(None, 'ws')
    in_specs = (row_mat, cache_spec, cache_spec, cache_spec, cache_spec, row_vec, row_mat, P(None, None), row_vec,
                P(None), P(None), P(None), col_split, col_split, col_split, col_split, col_split, col_split,
                col_split, P(None, None, 'ws'), P(None, 'ws', None))
    out_specs = (row_mat, cache_spec, cache_spec)

    def decoder_block(hidden, self_k, self_v, cross_k, cross_v, positions, enc_mask, rel_bias, expert_idx,
                      ln_self, ln_cross, ln_ffn, wq_self, wk_self, wv_self, wo_self, wq_cross, wo_cross,
                      w_router, w_in, w_out):
        rows, width = hidden.shape
        heads, length, head_dim = self_k.shape[1:]
        src_len = cross_k.shape[2]
        share = width // n
        heads_pad = -(-heads // 16) * 16
        experts, _, units = w_in.shape
        capacity = (2 * rows * n + experts - 1) // experts
        steps = rows // UNROLL
        chunk = 256

        def flat(cache):
            return jnp.swapaxes(cache, 2, 3).reshape(rows, width, cache.shape[2])

        dma = pltpu.SemaphoreType.DMA
        vmem, big_cache, big_src = pltpu.VMEM, (rows, width, length), (rows, width, src_len)
        ctx, kv, wall, router, e_all, k_v, v_v, ck_v, cv_v, win_v, wout_v = pl.pallas_call(
            functools.partial(self_kernel, n, head_dim),
            out_shape=(vmem((rows, width), BF16), vmem((2, rows, width), F32), vmem((n, 3 * share, width), BF16),
                       vmem((n, 1, width), F32), vmem((n, 1, 128), jnp.int32), vmem(big_cache, BF16),
                       vmem(big_cache, BF16), vmem(big_src, BF16), vmem(big_src, BF16), vmem(w_in.shape, BF16),
                       vmem(w_out.shape, BF16)),
            in_specs=[SM, SM] + [HBM] * 16,
            out_specs=(VM,) * 11,
            scratch_shapes=[
                vmem((n, rows, width), BF16), vmem((width,), F32), vmem((heads, length), F32),
                vmem((3, share, width), BF16), vmem((n * rows, 384), BF16), vmem((n, rows, 384), BF16),
                vmem((rows, width), F32), vmem((rows, heads_pad, length), F32), vmem((rows, heads_pad, length), BF16),
                vmem((rows, width), F32), vmem((heads_pad, length), F32),
                dma((10,)), dma((steps,)), dma((steps,)), dma((4,)), dma((7,)), dma((n,)), dma((7,)), dma((n,)),
                dma((7,)), dma((n,)), dma((7,)), dma((n,)), dma((28,)), dma((n, 4)),
            ],
            compiler_params=pltpu.CompilerParams(collective_id=0, has_side_effects=True,
                                                 vmem_limit_bytes=8 * 2 ** 20),
            name='self_part',
        )(positions, expert_idx,
          *in_hbm(hidden, ln_self, rel_bias, w_router.T, wq_self.T, wk_self.T, wv_self.T, wo_self.T, wq_cross.T,
                  wo_cross.T, flat(self_k), flat(self_v), flat(cross_k), flat(cross_v), w_in, w_out))

        newk, newv, h1, ctx2 = pl.pallas_call(
            functools.partial(cross_kernel, head_dim),
            out_shape=(pltpu.HBM(big_cache, BF16), pltpu.HBM(big_cache, BF16), vmem((rows, width), F32),
                       vmem((rows, width), BF16)),
            in_specs=[SM, VM, VM, VM, HBM, HBM, HBM, VM, VM, VM, VM],
            out_specs=(HBM, HBM, VM, VM),
            scratch_shapes=[
                vmem((rows, width), BF16), vmem((width,), F32), vmem((rows, src_len), jnp.int32), vmem((width, 128), F32),
                vmem((width, 128), F32), vmem((rows, width, 128), BF16), vmem((rows, width, 128), BF16),
                vmem((rows, width), F32), vmem((rows, heads_pad, src_len), F32), vmem((rows, heads_pad, src_len), BF16),
                vmem((rows, width), F32),
                dma((3,)), dma((rows, length // 128)), dma((rows, length // 128)),
            ],
            compiler_params=pltpu.CompilerParams(has_side_effects=True, vmem_limit_bytes=12 * 2 ** 20),
            name='cross_part',
        )(positions, *in_vmem(kv, ctx, wall), *in_hbm(hidden, ln_cross, enc_mask), *in_vmem(k_v, v_v, ck_v, cv_v))

        out = pl.pallas_call(
            functools.partial(ffn_kernel, n, capacity),
            out_shape=jax.ShapeDtypeStruct((rows, width), BF16),
            in_specs=[VM] * 5 + [HBM] + [VM] * 2,
            out_specs=VM,
            scratch_shapes=[
                vmem((width,), F32), vmem((n, rows, width), BF16), vmem((experts, n * rows, units), BF16),
                vmem((width // chunk, n * rows, chunk), F32), vmem((n, width // chunk, rows, chunk), F32),
                dma((1,)), dma((7,)), dma((n,)), dma((width // chunk, 7)), dma((width // chunk, n)),
            ],
            compiler_params=pltpu.CompilerParams(collective_id=1, has_side_effects=True,
                                                 vmem_limit_bytes=12 * 2 ** 20),
            name='ffn_part',
        )(*in_vmem(h1, ctx2, wall, router, e_all), *in_hbm(ln_ffn), *in_vmem(win_v, wout_v))

        def unflat(cache):
            return jnp.swapaxes(cache.reshape(rows, heads, head_dim, length), 2, 3)
        return out, unflat(newk), unflat(newv)

    return jax.shard_map(decoder_block, mesh=mesh, in_specs=in_specs, out_specs=out_specs, check_vma=False)
```

time: 61.8 us -> 55.6 us (0.90)
  Pallas kernels: 60.3 us -> 52.9 us
  local copies, waits for them, and re-layouts: 0.62 us -> 1.92 us
    pallas_call x3, Pallas kernels: 60.3 us -> 52.9 us  [the longest x1 27.6 us: decoder_block(): pl.pallas_call(functools.partial(self_kernel, n, head_dim), out_shape=(vm...]
    unnamed x5 -> x7, local copies, waits for them, and re-layouts: 0.62 us -> 1.92 us
where the time goes in v3:
time: 55.6 us; the launch traced here: 55.5 us
  Pallas kernels  52.9 us (95%)
  local copies, waits for them, and re-layouts  1.92 us (3%)
  between operations  0.68 us (1%)
    pallas_call x1, Pallas kernels, decoder_block(): pl.pallas_call(functools.partial(self_kernel, n, head_dim), out_shape=(vm...  27.6 us
    pallas_call x1, Pallas kernels, decoder_block(): pl.pallas_call(functools.partial(ffn_kernel, n, capacity), out_shape=jax....  15.8 us
    pallas_call x1, Pallas kernels, decoder_block(): pl.pallas_call(functools.partial(cross_kernel, head_dim), out_shape=(pltp...  9.43 us
    unnamed x7, local copies, waits for them, and re-layouts  1.92 us

profile of v3, /device:TPU:81, one launch (start us, length us, event | category | flops | bytes accessed | tf_op | source)
XLA Modules:
  0.0 55.5 jit_solution(5717722302453020115)
XLA Ops:
  0.6 0.0 copy-start
  0.6 0.6 %copy-done = s32[16]{0:T(128)S(1)} copy-done((s32[16]{0:T(128)S(1)}, s32[16]{0:T(128)}, u32[]{:S(2)}) %copy-start) | copy-done | bytes 88
  1.3 0.0 copy-start.2
  1.3 0.7 %copy-done.2 = s32[16]{0:T(128)S(1)} copy-done((s32[16]{0:T(128)S(1)}, s32[16]{0:T(128)}, u32[]{:S(2)}) %copy-start.2) | copy-done | bytes 88
  2.0 0.0 copy-start.1
  2.0 27.6 %self_part.1 = (bf16[16,768]{1,0:T(8,128)(2,1)S(1)}, f32[2,16,768]{2,1,0:T(8,128)S(1)}, bf16[8,288,768]{2,1,0:T(8,128)(2,1)S(1)}, f32[8,1,768]{2,1,0:T(1,128)S(1...) custom-call(s32[16]{0:T(128)S(1)} %copy-done, ...), custom_call_target="tpu_custom_call" | custom-call | tf_op jit(solution)/shard_map/self_part/pallas_call | solution.py:445
  29.6 0.0 copy-done.1
  29.6 9.4 %cross_part.1 = (bf16[16,768,384]{2,1,0:T(8,128)(2,1)}, bf16[16,768,384]{2,1,0:T(8,128)(2,1)}, f32[16,768]{1,0:T(8,128)S(1)}, bf16[16,768]{1,0:T(8,128)(2,1)S(1)}) custom-call(s32[16]{0:T(128)S(1)} %copy-done.1, f32[2,16,768]{2,1,0:T(8,128)S(1)} %get-tuple-element.18.kv_ref, bf16[16,768]{1,0:T(8,128)(2,1)S(1)} %get-tuple-element.19.ctx_ref, ...), custom_call_target="tpu_custom_call" | custom-call | tf_op jit(solution)/shard_map/cross_part/pallas_call | solution.py:468
  39.0 15.8 %ffn_part.1 = bf16[16,768]{1,0:T(8,128)(2,1)S(1)} custom-call(f32[16,768]{1,0:T(8,128)S(1)} %get-tuple-element.25.h1_ref, bf16[16,768]{1,0:T(8,128)(2,1)S(1)} %get-tuple-element.26.ctx2_ref, bf16[8,288,768]{2,1,0:T(8,128)(2,1)S(1)} %get-tuple-element.20.wall_ref, f32[8,1,768]{2,1,0:T(1,128)S(1)} %get-tuple-element.27.wr_ref, ...), custom_call_target="tpu_custom_call" | custom-call | tf_op jit(solution)/shard_map/ffn_part/pallas_call | solution.py:485
  54.9 0.6 %copy.25 = bf16[16,768]{1,0:T(8,128)(2,1)} copy(bf16[16,768]{1,0:T(8,128)(2,1)S(1)} %ffn_part.1) | data formatting | bytes 49152
Async XLA Ops:
  0.6 0.7 %copy-start = (s32[16]{0:T(128)S(1)}, s32[16]{0:T(128)}, u32[]{:S(2)}) copy-start(s32[16]{0:T(128)} %pos_ref.3) | copy-start | bytes 196
  1.3 0.7 %copy-start.2 = (s32[16]{0:T(128)S(1)}, s32[16]{0:T(128)}, u32[]{:S(2)}) copy-start(s32[16]{0:T(128)} %eidx_ref.1) | copy-start | bytes 196
  2.0 27.6 %copy-start.1 = (s32[16]{0:T(128)S(1)}, s32[16]{0:T(128)}, u32[]{:S(2)}) copy-start(s32[16]{0:T(128)} %pos_ref.3) | copy-start | bytes 196

commit v4 on v0

v4 whole, which is shorter than its diff:
```python
import functools
import jax
import jax.numpy as jnp
from jax import lax
from jax.experimental import pallas as pl
from jax.experimental.pallas import tpu as pltpu
from jax.sharding import PartitionSpec as P

EPSILON = 1e-6
NEG_BIG = -1e30
F32, BF16 = jnp.float32, jnp.bfloat16
MESH = pl.DeviceIdType.MESH
VM = pl.BlockSpec(memory_space=pltpu.VMEM)
HBM = pl.BlockSpec(memory_space=pltpu.HBM)
NT = (((1,), (1,)), ((), ()))
FROM_LEFT, FROM_RIGHT, FROM_FAR = 0, 1, 2
PEERS = ((2, 0), (2, 1), (1, 0), (3, 0), (1, 1), (3, 1), (0, 1))
UNROLL = 4


def in_hbm(*arrays):
    return [pltpu.with_memory_space_constraint(a, pltpu.HBM) for a in arrays]


def in_vmem(*arrays):
    return [pltpu.with_memory_space_constraint(a, pltpu.VMEM) for a in arrays]


def rms_norm(hid_f32, scale):
    inv_rms = lax.rsqrt(jnp.mean(hid_f32 * hid_f32, axis=-1, keepdims=True) + EPSILON)
    return (hid_f32 * inv_rms * scale).astype(BF16)


def dot_nt(a, b):
    return lax.dot_general(a, b, NT, preferred_element_type=F32)


def softmax_rows(scores):
    top = jnp.max(scores, axis=-1, keepdims=True)
    ex = jnp.exp(scores - top)
    return (ex / jnp.sum(ex, axis=-1, keepdims=True)).astype(BF16)


def make_dev(n):
    me = lax.axis_index('ws')
    chips = n // 2
    chip, core = me // 2, lax.rem(me, 2)

    def dev(step, other):
        return 2 * lax.rem(chip + step, chips) + ((1 - core) if other else core)
    return me, dev


def remote(src, dst, send_sem, recv_sem, dev):
    return pltpu.make_async_remote_copy(src_ref=src, dst_ref=dst, send_sem=send_sem, recv_sem=recv_sem,
                                        device_id={'ws': dev}, device_id_type=MESH)


def to_peers(dev, me, ref, send_sem, recv_sem):
    return [remote(ref.at[me], ref.at[me], send_sem, recv_sem, dev(*peer)) for peer in PEERS]


def all_of(ref, count, send_sem, recv_sem, dev):
    block = ref.at[pl.ds(0, count)]
    return remote(block, block, send_sem, recv_sem, dev)


def head_mask(heads_pad, width, head_dim):
    row = lax.broadcasted_iota(jnp.int32, (heads_pad, width), 0)
    col = lax.broadcasted_iota(jnp.int32, (heads_pad, width), 1)
    return (col // head_dim == row).astype(F32)


def main_kernel(n, head_dim, capacity, pos_hbm, eidx_hbm, hid_hbm, ln_hbm, lnc_hbm, lnf_hbm, rel_hbm, mask_hbm, wr_hbm,
                wq_hbm, wk_hbm, wv_hbm, wo_hbm, wqc_hbm, woc_hbm, k_hbm, v_hbm, ck_hbm, cv_hbm, win_hbm, wout_hbm,
                out_ref, k_ref, v_ref,
                ck_ref, cv_ref, win_ref, wout_ref, wall_ref, pos_ref, eidx_ref, ln_ref, lnc_ref, lnf_ref, rel_ref, mask_ref, wr_ref, eall_ref, xall_ref, yall_ref, hid_ref,
                wqkv_ref, qsend_ref, qrecv_ref, q_ref, kv_ref, kt_ref, vt_ref, s_ref, p_ref, s2_ref, p2_ref, ctx32_ref,
                rrev_ref, u_ref, part_ref, rs_ref,
                in_sem, big_sem, x_sem, r_sem, e_sem, q_sem, y_sem, w_send, w_recv, pair_recv, rs_send, rs_recv):
    me, dev = make_dev(n)
    rows, width, length = k_ref.shape
    heads_pad = s_ref.shape[1]
    share = width // n
    half = share // 2
    steps = rows // UNROLL
    peers = len(PEERS)
    pieces = ((0, share), (share, share), (2 * share, half), (2 * share + half, half))

    barrier = pltpu.get_barrier_semaphore()
    for peer in PEERS:
        pl.semaphore_signal(barrier, inc=1, device_id={'ws': dev(*peer)}, device_id_type=MESH)

    mine = wall_ref.at[me]
    loads = [
        (hid_hbm, xall_ref.at[me], 0), (wr_hbm, wr_ref.at[me], 1), (ln_hbm, ln_ref, 2), (wq_hbm, wqkv_ref.at[0], 3),
        (wk_hbm, wqkv_ref.at[1], 3), (wv_hbm, wqkv_ref.at[2], 3), (rel_hbm, rel_ref, 4),
        (wo_hbm, mine.at[pl.ds(0, share)], 5), (wqc_hbm, mine.at[pl.ds(share, share)], 5),
        (woc_hbm, mine.at[pl.ds(2 * share, share)], 5), (eidx_hbm, eidx_ref, 6), (pos_hbm, pos_ref, 7),
        (lnc_hbm, lnc_ref, 8), (lnf_hbm, lnf_ref, 9), (mask_hbm, mask_ref, 10), (hid_hbm, hid_ref, 11),
    ]
    loads = [pltpu.make_async_copy(src, dst, in_sem.at[i]) for src, dst, i in loads]
    for load in loads:
        load.start()
    experts = win_ref.shape[0]
    lane_id = lax.broadcasted_iota(jnp.int32, (1, 128), 1)
    loads[0].wait()
    pl.semaphore_wait(barrier, n - 1)
    for copy in to_peers(dev, me, xall_ref, x_sem.at[0], x_sem.at[1]):
        copy.start()
    pltpu.make_async_copy(mine, mine, in_sem.at[5]).wait()

    right, left, far, sib = dev(1, 0), dev(3, 0), dev(2, 0), dev(0, 1)

    def send_piece(owner, role, part, target):
        start, size = pieces[part]
        block = wall_ref.at[owner, pl.ds(start, size)]
        sem = pair_recv.at[part // 2] if role is None else w_recv.at[role, part]
        remote(block, block, w_send.at[0], sem, target).start()

    def wait_piece(owner, role, part):
        start, size = pieces[part]
        block = wall_ref.at[owner, pl.ds(start, size)]
        remote(block, block, w_send.at[0], w_recv.at[role, part], sib).wait_recv()

    def wait_pair(stage):
        size = 2 * share if stage == 0 else share
        block = wall_ref.at[pl.ds(0, n // 2), pl.ds(0, size)]
        remote(block, block, w_send.at[0], pair_recv.at[stage], sib).wait_recv()

    send_piece(me, FROM_LEFT, 0, right)
    send_piece(me, FROM_RIGHT, 1, left)
    loads[1].wait()
    loads[10].wait()
    e_row = jnp.zeros((1, 128), jnp.int32)
    for b in range(rows):
        e_row = jnp.where(lane_id == b, eidx_ref[b], e_row)
    eall_ref[me] = e_row
    big = [pltpu.make_async_copy(src, dst, big_sem.at[i]) for i, (src, dst) in
           enumerate([(k_hbm, k_ref), (v_hbm, v_ref), (ck_hbm, ck_ref), (cv_hbm, cv_ref), (win_hbm, win_ref), (wout_hbm, wout_ref)])]
    for load in big:
        load.start()

    loads[6].wait()
    rel = jnp.concatenate([rel_ref[...], jnp.zeros((heads_pad - rel_ref.shape[0], length), F32)], axis=0)
    flip = (lax.broadcasted_iota(jnp.int32, (length, length), 0) + lax.broadcasted_iota(jnp.int32, (length, length), 1)
            == length - 1).astype(F32).astype(BF16)
    hi = rel.astype(BF16)
    rest = rel - hi.astype(F32)
    mid = rest.astype(BF16)
    low = (rest - mid.astype(F32)).astype(BF16)
    rrev_ref[...] = (jnp.dot(hi, flip, preferred_element_type=F32) + jnp.dot(mid, flip, preferred_element_type=F32)
                     + jnp.dot(low, flip, preferred_element_type=F32))
    qsend_ref[...] = jnp.zeros_like(qsend_ref)

    for load in loads[2:3] + loads[11:]:
        load.wait()
    pltpu.make_async_copy(wqkv_ref, wqkv_ref, in_sem.at[3]).wait()
    all_of(xall_ref, peers, x_sem.at[0], x_sem.at[1], sib).wait_recv()
    x_norm = rms_norm(xall_ref[...].reshape(n * rows, width).astype(F32), ln_ref[...][None])
    for part in range(3):
        qsend_ref[:, part * 128:part * 128 + share] = dot_nt(x_norm, wqkv_ref[part]).astype(BF16)
    for peer in PEERS:
        dst = dev(*peer)
        remote(qsend_ref.at[pl.ds(dst * rows, rows)], qrecv_ref.at[me], q_sem.at[0], q_sem.at[1], dst).start()
    qrecv_ref[me] = qsend_ref[pl.ds(pl.multiple_of(me * rows, rows), rows), :]
    send_piece(me, FROM_LEFT, 1, right)
    send_piece(me, FROM_RIGHT, 0, left)
    for part in range(len(pieces)):
        send_piece(me, None, part, sib)
    for copy in (to_peers(dev, me, wr_ref, r_sem.at[0], r_sem.at[1])
                 + to_peers(dev, me, eall_ref, e_sem.at[0], e_sem.at[1])):
        copy.start()

    all_of(qrecv_ref, peers, q_sem.at[0], q_sem.at[1], sib).wait_recv()
    wait_piece(left, FROM_LEFT, 0)
    send_piece(left, FROM_FAR, 0, right)
    wait_piece(right, FROM_RIGHT, 1)
    send_piece(right, FROM_FAR, 1, left)
    for part in (2, 3):
        send_piece(me, FROM_LEFT, part, right)
        send_piece(me, FROM_RIGHT, 5 - part, left)
    send_piece(left, None, 0, sib)
    send_piece(right, None, 1, sib)

    def columns(part):
        return jnp.concatenate([qrecv_ref[s][:, part * 128:part * 128 + share] for s in range(n)], axis=1).astype(F32)
    q_ref[...] = columns(0)
    kv_ref[0] = columns(1)
    kv_ref[1] = columns(2)

    h_mask = head_mask(heads_pad, width, head_dim)
    lane = lax.broadcasted_iota(jnp.int32, (1, length), 1)

    big[0].wait()

    def score_step(i, carry):
        for s in range(UNROLL):
            b = i * UNROLL + s
            pos = pos_ref[b]
            q_diag = q_ref[pl.ds(b, 1), :] * h_mask
            scores = jnp.dot(q_diag.astype(BF16), k_ref[b], preferred_element_type=F32)
            new = jnp.sum(q_diag * kv_ref[0, pl.ds(b, 1), :], axis=1, keepdims=True)
            bias = pltpu.roll(rrev_ref[...], pos + 1, axis=1)
            s_ref[b] = jnp.where(lane <= pos, jnp.where(lane == pos, new, scores) + bias, NEG_BIG)
        return carry
    lax.fori_loop(0, steps, score_step, 0)

    p_ref[...] = softmax_rows(s_ref[...])

    big[1].wait()

    def value_step(i, carry):
        for s in range(UNROLL):
            b = i * UNROLL + s
            here = lane == pos_ref[b]
            probs = p_ref[b].astype(F32)
            new = jnp.sum(jnp.where(here, probs, 0.0), axis=1, keepdims=True)
            spread = dot_nt(jnp.where(here, 0.0, probs).astype(BF16), v_ref[b])
            spread = spread + new * kv_ref[1, pl.ds(b, 1), :]
            ctx32_ref[pl.ds(b, 1), :] = jnp.sum(spread * h_mask, axis=0, keepdims=True)
        return carry
    lax.fori_loop(0, steps // 2, value_step, 0)
    for owner, role, part in ((left, FROM_LEFT, 1), (right, FROM_RIGHT, 0)):
        wait_piece(owner, role, part)
        send_piece(owner, None, part, sib)
    lax.fori_loop(steps // 2, steps, value_step, 0)

    for part in (0, 1):
        wait_piece(far, FROM_FAR, part)
        send_piece(far, None, part, sib)
    wait_pair(0)

    wo = wall_ref[:, 0:share, :].reshape(width, width)
    h1 = (hid_ref[...].astype(F32) + dot_nt(ctx32_ref[...].astype(BF16), wo)).astype(BF16).astype(F32)
    wqc = wall_ref[:, share:2 * share, :].reshape(width, width)
    q_ref[...] = dot_nt(rms_norm(h1, lnc_ref[...][None]), wqc).astype(BF16).astype(F32)
    wait_piece(left, FROM_LEFT, 2)
    send_piece(left, FROM_FAR, 2, right)
    wait_piece(right, FROM_RIGHT, 3)
    send_piece(right, FROM_FAR, 3, left)
    send_piece(left, None, 2, sib)
    send_piece(right, None, 3, sib)
    for load in big[2:]:
        load.wait()

    def cross_score(i, carry):
        for s in range(UNROLL):
            b = i * UNROLL + s
            q_diag = (q_ref[pl.ds(b, 1), :] * h_mask).astype(BF16)
            scores = jnp.dot(q_diag, ck_ref[b], preferred_element_type=F32)
            s2_ref[b] = jnp.where(mask_ref[pl.ds(b, 1), :] == 1, scores, NEG_BIG)
        return carry
    lax.fori_loop(0, steps, cross_score, 0)
    for owner, role, part in ((left, FROM_LEFT, 3), (right, FROM_RIGHT, 2)):
        wait_piece(owner, role, part)
        send_piece(owner, None, part, sib)
    p2_ref[...] = softmax_rows(s2_ref[...])

    def cross_value(i, carry):
        for s in range(UNROLL):
            b = i * UNROLL + s
            spread = dot_nt(p2_ref[b], cv_ref[b])
            ctx32_ref[pl.ds(b, 1), :] = jnp.sum(spread * h_mask, axis=0, keepdims=True)
        return carry
    lax.fori_loop(0, steps, cross_value, 0)

    for part in (2, 3):
        wait_piece(far, FROM_FAR, part)
        send_piece(far, None, part, sib)
    wait_pair(1)
    woc = wall_ref[:, 2 * share:3 * share, :].reshape(width, width)
    h2 = (h1 + dot_nt(ctx32_ref[...].astype(BF16), woc)).astype(BF16).astype(F32)
    x_own = rms_norm(h2, lnf_ref[...][None])
    yall_ref[me] = x_own
    for copy in to_peers(dev, me, yall_ref, y_sem.at[0], y_sem.at[1]):
        copy.start()

    all_of(wr_ref, peers, r_sem.at[0], r_sem.at[1], sib).wait_recv()
    all_of(eall_ref, peers, e_sem.at[0], e_sem.at[1], sib).wait_recv()
    x_f32 = x_own.astype(F32)
    logits = [jnp.sum(x_f32 * wr_ref[e], axis=-1, keepdims=True) for e in range(experts)]
    top = functools.reduce(jnp.maximum, logits)
    ex = [jnp.exp(v - top) for v in logits]
    total = functools.reduce(jnp.add, ex)
    e_pad = jnp.concatenate([eall_ref[...].reshape(n, 128), jnp.zeros((128 - n, 128), jnp.int32)], axis=0)
    e_cols = e_pad.astype(F32).T.astype(jnp.int32)
    e_all = jnp.concatenate([jnp.broadcast_to(e_cols[0:rows, s:s + 1], (rows, 128)) for s in range(n)], axis=0)
    row_id = lax.broadcasted_iota(jnp.int32, (rows, 128), 1)
    source = lax.broadcasted_iota(jnp.int32, (rows, 128), 1)
    e_own = jnp.sum(jnp.where(source == me, e_cols[0:rows, :], 0).astype(F32), axis=1, keepdims=True).astype(jnp.int32)
    gate = functools.reduce(jnp.add, [jnp.where(e_own == e, ex[e], 0.0) for e in range(experts)]) / total
    one_hot = (e_all == lax.broadcasted_iota(jnp.int32, (n * rows, 128), 1)).astype(F32).astype(BF16)
    earlier = (lax.broadcasted_iota(jnp.int32, (rows, n * rows), 1)
               < me * rows + lax.broadcasted_iota(jnp.int32, (rows, n * rows), 0)).astype(F32).astype(BF16)
    counts = jnp.dot(earlier, one_hot, preferred_element_type=F32)
    slot = jnp.sum(jnp.where(row_id == e_own, counts, 0.0), axis=-1, keepdims=True)
    keep_gate = jnp.where(slot < capacity, gate, 0.0)

    pad = jnp.zeros((128 - rows, width), F32)
    kt_ref[...] = jnp.concatenate([kv_ref[0], pad], axis=0).T
    vt_ref[...] = jnp.concatenate([kv_ref[1], pad], axis=0).T

    def patch_row(b, column, cache_ref):
        cache_ref[b] = jnp.where(lane == pos_ref[b], jnp.broadcast_to(column, (width, length)).astype(BF16), cache_ref[b])

    def patch_step(i, carry):
        kt = kt_ref[...]
        vt = vt_ref[...]
        for s in range(UNROLL):
            patch_row(i * UNROLL + s, kt[:, s:s + 1], k_ref)
            patch_row(i * UNROLL + s, vt[:, s:s + 1], v_ref)
        kt_ref[...] = pltpu.roll(kt, 128 - UNROLL, axis=1)
        vt_ref[...] = pltpu.roll(vt, 128 - UNROLL, axis=1)
        return carry
    lax.fori_loop(0, steps, patch_step, 0)

    all_of(yall_ref, peers, y_sem.at[0], y_sem.at[1], sib).wait_recv()
    x_all = yall_ref[...].reshape(n * rows, width)
    e_wide = jnp.concatenate([e_all] * (win_ref.shape[2] // 128), axis=1)

    def expert_step(e, carry):
        u = jnp.maximum(jnp.dot(x_all, win_ref[e], preferred_element_type=F32), 0.0)
        u_ref[e] = jnp.where(e_wide == e, u, 0.0).astype(BF16)
        return carry
    lax.fori_loop(0, experts, expert_step, 0)

    chunk = part_ref.shape[2]
    for c in range(width // chunk):
        acc = jnp.zeros((n * rows, chunk), F32)
        for e in range(experts):
            acc = acc + jnp.dot(u_ref[e], wout_ref[e, :, c * chunk:(c + 1) * chunk], preferred_element_type=F32)
        part_ref[c] = acc
        rs_ref[c, me] = part_ref[c, pl.ds(pl.multiple_of(me * rows, rows), rows), :]
        for peer in PEERS:
            dst = dev(*peer)
            remote(part_ref.at[c, pl.ds(dst * rows, rows)], rs_ref.at[c, me], rs_send.at[0], rs_recv.at[c], dst).start()
    for c in range(width // chunk):
        all_of(rs_ref.at[c], peers, rs_send.at[0], rs_recv.at[c], sib).wait_recv()
        y = jnp.sum(rs_ref[c], axis=0).astype(BF16).astype(F32)
        cols = slice(c * chunk, (c + 1) * chunk)
        out_ref[:, cols] = (h2[:, cols] + y * keep_gate).astype(BF16)
    for ref, sem in ((xall_ref, x_sem), (qrecv_ref, q_sem), (yall_ref, y_sem), (wr_ref, r_sem), (eall_ref, e_sem),
                     (wall_ref, w_send)):
        all_of(ref, peers, sem.at[0], sem.at[0], sib).wait_send()
    sent = rs_ref.at[:, pl.ds(0, peers)]
    remote(sent, sent, rs_send.at[0], rs_send.at[0], sib).wait_send()


def write_kernel(hid_ref, k_ref, v_ref, out_hbm, newk_hbm, newv_hbm, sem):
    span = k_ref.shape[0] // 4
    copies = [pltpu.make_async_copy(hid_ref, out_hbm, sem.at[8])]
    for i in range(4):
        rows = pl.ds(i * span, span)
        copies.append(pltpu.make_async_copy(k_ref.at[rows], newk_hbm.at[rows], sem.at[2 * i]))
        copies.append(pltpu.make_async_copy(v_ref.at[rows], newv_hbm.at[rows], sem.at[2 * i + 1]))
    for copy in copies:
        copy.start()
    for copy in copies:
        copy.wait()


def solution(mesh):
    n = mesh.shape['ws']
    row_axes = ('dp', 'ws')
    row_vec = P(row_axes)
    row_mat = P(row_axes, None)
    cache_spec = P(row_axes, None, None, None)
    col_split = P(None, 'ws')
    in_specs = (row_mat, cache_spec, cache_spec, cache_spec, cache_spec, row_vec, row_mat, P(None, None), row_vec,
                P(None), P(None), P(None), col_split, col_split, col_split, col_split, col_split, col_split,
                col_split, P(None, None, 'ws'), P(None, 'ws', None))
    out_specs = (row_mat, cache_spec, cache_spec)

    def decoder_block(hidden, self_k, self_v, cross_k, cross_v, positions, enc_mask, rel_bias, expert_idx,
                      ln_self, ln_cross, ln_ffn, wq_self, wk_self, wv_self, wo_self, wq_cross, wo_cross,
                      w_router, w_in, w_out):
        rows, width = hidden.shape
        heads, length, head_dim = self_k.shape[1:]
        src_len = cross_k.shape[2]
        share = width // n
        heads_pad = -(-heads // 16) * 16
        experts, _, units = w_in.shape
        capacity = (2 * rows * n + experts - 1) // experts
        chunk = 256

        def flat(cache):
            return jnp.swapaxes(cache, 2, 3).reshape(rows, width, cache.shape[2])

        dma = pltpu.SemaphoreType.DMA
        vmem, big_cache, big_src = pltpu.VMEM, (rows, width, length), (rows, width, src_len)
        parts, smem = width // chunk, pltpu.SMEM
        hid_out, k_v, v_v = pl.pallas_call(
            functools.partial(main_kernel, n, head_dim, capacity),
            out_shape=(vmem((rows, width), BF16), vmem(big_cache, BF16), vmem(big_cache, BF16)),
            in_specs=[HBM] * 21,
            out_specs=(VM,) * 3,
            scratch_shapes=[
                vmem(big_src, BF16), vmem(big_src, BF16), vmem(w_in.shape, BF16), vmem(w_out.shape, BF16),
                vmem((n, 3 * share, width), BF16),
                smem((rows,), jnp.int32), smem((rows,), jnp.int32), vmem((width,), F32), vmem((width,), F32),
                vmem((width,), F32), vmem((heads, length), F32), vmem((rows, src_len), jnp.int32),
                vmem((n, 1, width), F32), vmem((n, 1, 128), jnp.int32), vmem((n, rows, width), BF16),
                vmem((n, rows, width), BF16), vmem((rows, width), BF16), vmem((3, share, width), BF16),
                vmem((n * rows, 384), BF16), vmem((n, rows, 384), BF16), vmem((rows, width), F32),
                vmem((2, rows, width), F32), vmem((width, 128), F32), vmem((width, 128), F32),
                vmem((rows, heads_pad, length), F32), vmem((rows, heads_pad, length), BF16),
                vmem((rows, heads_pad, src_len), F32), vmem((rows, heads_pad, src_len), BF16), vmem((rows, width), F32),
                vmem((heads_pad, length), F32), vmem((experts, n * rows, units), BF16),
                vmem((parts, n * rows, chunk), F32), vmem((parts, n, rows, chunk), F32),
                dma((12,)), dma((6,)), dma((2,)), dma((2,)), dma((2,)), dma((2,)), dma((2,)), dma((1,)), dma((3, 4)),
                dma((2,)), dma((1,)), dma((parts,)),
            ],
            compiler_params=pltpu.CompilerParams(collective_id=0, has_side_effects=True,
                                                 vmem_limit_bytes=34 * 2 ** 20),
            name='main_part',
        )(*in_hbm(positions, expert_idx, hidden, ln_self, ln_cross, ln_ffn, rel_bias, enc_mask, w_router.T, wq_self.T,
                  wk_self.T, wv_self.T, wo_self.T, wq_cross.T, wo_cross.T, flat(self_k), flat(self_v), flat(cross_k),
                  flat(cross_v), w_in, w_out))

        out, newk, newv = pl.pallas_call(
            write_kernel,
            out_shape=(pltpu.HBM((rows, width), BF16), pltpu.HBM(big_cache, BF16), pltpu.HBM(big_cache, BF16)),
            in_specs=[VM] * 3,
            out_specs=(HBM,) * 3,
            scratch_shapes=[dma((9,))],
            compiler_params=pltpu.CompilerParams(has_side_effects=True, vmem_limit_bytes=2 ** 20),
            name='write_part',
        )(*in_vmem(hid_out, k_v, v_v))

        def unflat(cache):
            return jnp.swapaxes(cache.reshape(rows, heads, head_dim, length), 2, 3)
        return out, unflat(newk), unflat(newv)

    return jax.shard_map(decoder_block, mesh=mesh, in_specs=in_specs, out_specs=out_specs, check_vma=False)
```

time: 594 us -> 49.6 us (0.08)
  waiting for transfers between devices: 285 us -> 0 us
  local copies, waits for them, and re-layouts: 168 us -> 0 us
  matrix products: 80.6 us -> 0 us
  Pallas kernels: 0 us -> 48.9 us
  blocking collectives: 23.8 us -> 0 us
  other arithmetic: 20.1 us -> 0 us
  between operations: 15.2 us -> 0.65 us
    all_gather x8 -> x0, waiting for transfers between devices: 280 us -> none  [the longest x1 171 us: decoder_block(): win_full = gather_ws(w_in, axis=2)]
    gather x9 -> x0, local copies, waits for them, and re-layouts: 158 us -> none  [the longest x4 69.2 us: decoder_block(): jnp.take(wout_full, expert_idx, axis=0)]
    dot_general x13 -> x0, matrix products: 80.6 us -> none  [the longest x1 27.4 us: decoder_block(): jnp.einsum('bd,bdf->bf', x_norm, jnp.take(win_full, expert_idx, axis=0),...]
    pallas_call x0 -> x2, Pallas kernels: none -> 48.9 us  [the longest x1 42.3 us: decoder_block(): pl.pallas_call(functools.partial(main_kernel, n, head_dim, capacity), out...]
    all_gather x1 -> x0, blocking collectives: 14.9 us -> none  [decoder_block(): router_full = gather_ws(w_router, axis=1)]
    select_n x5 -> x0, other arithmetic: 13.5 us -> none  [the longest x1 12.2 us: decoder_block(): new_self_v = jnp.where(write_mask, v_new[:, :, None, :], self_v)]
    unnamed x1 -> x0, blocking collectives: 8.95 us -> none
  transfers between devices with their start and end apart: 8 -> 0, of which waited for: 5 -> 0; matrix products, arithmetic and copies ran while one was open for 29% -> 0% of each run, Pallas kernels for 0% -> 0%
where the time goes in v4:
time: 49.6 us; the launch traced here: 49.5 us
  Pallas kernels  48.9 us (99%)
  between operations  0.65 us (1%)
    pallas_call x1, Pallas kernels, decoder_block(): pl.pallas_call(functools.partial(main_kernel, n, head_dim, capacity), out...  42.3 us
    pallas_call x1, Pallas kernels, decoder_block(): pl.pallas_call(write_kernel, out_shape=(pltpu.HBM((rows, width), BF16), p...  6.6 us

profile of v4, /device:TPU:81, one launch (start us, length us, event | category | flops | bytes accessed | tf_op | source)
XLA Modules:
  0.0 49.5 jit_solution(2121552716596783667)
XLA Ops:
  0.6 42.3 %main_part.1 = (bf16[16,768]{1,0:T(8,128)(2,1)S(1)}, bf16[16,768,384]{2,1,0:T(8,128)(2,1)S(1)}, bf16[16,768,384]{2,1,0:T(8,128)(2,1)S(1)}) custom-call(s32[16]{0:T(128)} %pos_hbm.1, s32[16]{0:T(128)} %eidx_hbm.1, bf16[16,768]{1,0:T(8,128)(2,1)} %hid_hbm.1, f32[768]{0:T(1024)} %ln_hbm.1, f32[768]{0:T(1024)} %lnc_hbm.1, f32[768]{0:T(1024)} %lnf_hbm.1, ...), custom_call_target="tpu_custom_call" | custom-call | tf_op jit(solution)/shard_map/main_part/pallas_call | solution.py:393
  42.9 6.6 %write_part.1 = (bf16[16,768]{1,0:T(8,128)(2,1)}, bf16[16,768,384]{2,1,0:T(8,128)(2,1)}, bf16[16,768,384]{2,1,0:T(8,128)(2,1)}) custom-call(bf16[16,768]{1,0:T(8,128)(2,1)S(1)} %get-tuple-element.9.hid_ref, bf16[16,768,384]{2,1,0:T(8,128)(2,1)S(1)} %get-tuple-element.10.k_ref, bf16[16,768,384]{2,1,0:T(8,128)(2,1)S(1)} %get-tuple-element.11.v_ref), custom_call_target="tpu_custom_call" | custom-call | tf_op jit(solution)/shard_map/write_part/pallas_call | solution.py:421

commit v5 on v4

--- a/solution.py
+++ b/solution.py
@@ -76,8 +76,8 @@
                 out_ref, k_ref, v_ref,
                 ck_ref, cv_ref, win_ref, wout_ref, wall_ref, pos_ref, eidx_ref, ln_ref, lnc_ref, lnf_ref, rel_ref, mask_ref, wr_ref, eall_ref, xall_ref, yall_ref, hid_ref,
                 wqkv_ref, qsend_ref, qrecv_ref, q_ref, kv_ref, kt_ref, vt_ref, s_ref, p_ref, s2_ref, p2_ref, ctx32_ref,
-                rrev_ref, u_ref, part_ref, rs_ref,
-                in_sem, big_sem, x_sem, r_sem, e_sem, q_sem, y_sem, w_send, w_recv, pair_recv, rs_send, rs_recv):
+                rrev_ref, u_ref, part_ref, pair_ref, pair_sum_ref, rs_ref,
+                in_sem, big_sem, x_sem, r_sem, e_sem, q_sem, y_sem, w_send, w_recv, pair_recv, d_send, d_recv, rs_send, rs_recv):
     me, dev = make_dev(n)
     rows, width, length = k_ref.shape
     heads_pad = s_ref.shape[1]
@@ -231,16 +231,16 @@
         send_piece(far, None, part, sib)
     wait_pair(0)
 
-    wo = wall_ref[:, 0:share, :].reshape(width, width)
-    h1 = (hid_ref[...].astype(F32) + dot_nt(ctx32_ref[...].astype(BF16), wo)).astype(BF16).astype(F32)
-    wqc = wall_ref[:, share:2 * share, :].reshape(width, width)
-    q_ref[...] = dot_nt(rms_norm(h1, lnc_ref[...][None]), wqc).astype(BF16).astype(F32)
     wait_piece(left, FROM_LEFT, 2)
     send_piece(left, FROM_FAR, 2, right)
     wait_piece(right, FROM_RIGHT, 3)
     send_piece(right, FROM_FAR, 3, left)
     send_piece(left, None, 2, sib)
     send_piece(right, None, 3, sib)
+    wo = wall_ref[:, 0:share, :].reshape(width, width)
+    h1 = (hid_ref[...].astype(F32) + dot_nt(ctx32_ref[...].astype(BF16), wo)).astype(BF16).astype(F32)
+    wqc = wall_ref[:, share:2 * share, :].reshape(width, width)
+    q_ref[...] = dot_nt(rms_norm(h1, lnc_ref[...][None]), wqc).astype(BF16).astype(F32)
     for load in big[2:]:
         load.wait()
 
@@ -317,34 +317,42 @@
 
     all_of(yall_ref, peers, y_sem.at[0], y_sem.at[1], sib).wait_recv()
     x_all = yall_ref[...].reshape(n * rows, width)
-    e_wide = jnp.concatenate([e_all] * (win_ref.shape[2] // 128), axis=1)
-
-    def expert_step(e, carry):
-        u = jnp.maximum(jnp.dot(x_all, win_ref[e], preferred_element_type=F32), 0.0)
-        u_ref[e] = jnp.where(e_wide == e, u, 0.0).astype(BF16)
-        return carry
-    lax.fori_loop(0, experts, expert_step, 0)
-
-    chunk = part_ref.shape[2]
-    for c in range(width // chunk):
-        acc = jnp.zeros((n * rows, chunk), F32)
-        for e in range(experts):
-            acc = acc + jnp.dot(u_ref[e], wout_ref[e, :, c * chunk:(c + 1) * chunk], preferred_element_type=F32)
-        part_ref[c] = acc
-        rs_ref[c, me] = part_ref[c, pl.ds(pl.multiple_of(me * rows, rows), rows), :]
-        for peer in PEERS:
-            dst = dev(*peer)
-            remote(part_ref.at[c, pl.ds(dst * rows, rows)], rs_ref.at[c, me], rs_send.at[0], rs_recv.at[c], dst).start()
-    for c in range(width // chunk):
-        all_of(rs_ref.at[c], peers, rs_send.at[0], rs_recv.at[c], sib).wait_recv()
+    units = win_ref.shape[2]
+    e_wide = jnp.concatenate([e_all] * (2 * units // 128), axis=1)
+    second = (lax.broadcasted_iota(jnp.int32, (1, 2 * units), 1) >= units).astype(jnp.int32)
+    for e in range(0, experts, 2):
+        w_pair = jnp.concatenate([win_ref[e], win_ref[e + 1]], axis=1)
+        u = jnp.maximum(jnp.dot(x_all, w_pair, preferred_element_type=F32), 0.0)
+        u_ref[:, e * units:(e + 2) * units] = jnp.where(e_wide == e + second, u, 0.0).astype(BF16)
+
+    chunk = part_ref.shape[4]
+    parts = width // chunk
+    chip, core = me // 2, lax.rem(me, 2)
+    w_all = wout_ref.reshape(experts * units, width)
+    for c in range(parts):
+        acc = jnp.dot(u_ref[...], w_all[:, c * chunk:(c + 1) * chunk], preferred_element_type=F32)
+        part_ref[c] = acc.reshape(n // 2, 2, rows, chunk)
+        remote(part_ref.at[c, :, 1 - core], pair_ref.at[c], d_send.at[0], d_recv.at[c], sib).start()
+    for c in range(parts):
+        remote(pair_ref.at[c], pair_ref.at[c], d_send.at[0], d_recv.at[c], sib).wait_recv()
+        pair_sum_ref[c] = part_ref[c, :, core] + pair_ref[c]
+        rs_ref[c, chip] = pair_sum_ref[c, chip]
+        for step in (2, 1, 3):
+            target = lax.rem(chip + step, n // 2)
+            remote(pair_sum_ref.at[c, target], rs_ref.at[c, chip], rs_send.at[0], rs_recv.at[c],
+                   2 * target + core).start()
+    others = n // 2 - 1
+    for c in range(parts):
+        all_of(rs_ref.at[c], others, rs_send.at[0], rs_recv.at[c], sib).wait_recv()
         y = jnp.sum(rs_ref[c], axis=0).astype(BF16).astype(F32)
         cols = slice(c * chunk, (c + 1) * chunk)
         out_ref[:, cols] = (h2[:, cols] + y * keep_gate).astype(BF16)
     for ref, sem in ((xall_ref, x_sem), (qrecv_ref, q_sem), (yall_ref, y_sem), (wr_ref, r_sem), (eall_ref, e_sem),
                      (wall_ref, w_send)):
         all_of(ref, peers, sem.at[0], sem.at[0], sib).wait_send()
-    sent = rs_ref.at[:, pl.ds(0, peers)]
+    sent = rs_ref.at[:, pl.ds(0, others)]
     remote(sent, sent, rs_send.at[0], rs_send.at[0], sib).wait_send()
+    remote(pair_ref, pair_ref, d_send.at[0], d_send.at[0], sib).wait_send()
 
 
 def write_kernel(hid_ref, k_ref, v_ref, out_hbm, newk_hbm, newv_hbm, sem):
@@ -406,10 +414,11 @@
                 vmem((2, rows, width), F32), vmem((width, 128), F32), vmem((width, 128), F32),
                 vmem((rows, heads_pad, length), F32), vmem((rows, heads_pad, length), BF16),
                 vmem((rows, heads_pad, src_len), F32), vmem((rows, heads_pad, src_len), BF16), vmem((rows, width), F32),
-                vmem((heads_pad, length), F32), vmem((experts, n * rows, units), BF16),
-                vmem((parts, n * rows, chunk), F32), vmem((parts, n, rows, chunk), F32),
+                vmem((heads_pad, length), F32), vmem((n * rows, experts * units), BF16),
+                vmem((parts, n // 2, 2, rows, chunk), F32), vmem((parts, n // 2, rows, chunk), F32),
+                vmem((parts, n // 2, rows, chunk), F32), vmem((parts, n // 2, rows, chunk), F32),
                 dma((12,)), dma((6,)), dma((2,)), dma((2,)), dma((2,)), dma((2,)), dma((2,)), dma((1,)), dma((3, 4)),
-                dma((2,)), dma((1,)), dma((parts,)),
+                dma((2,)), dma((1,)), dma((parts,)), dma((1,)), dma((parts,)),
             ],
             compiler_params=pltpu.CompilerParams(collective_id=0, has_side_effects=True,
                                                  vmem_limit_bytes=34 * 2 ** 20),

time: 49.6 us -> 47.2 us (0.952)
  Pallas kernels: 48.9 us -> 46.5 us
    pallas_call x1, Pallas kernels: 42.3 us -> 39.9 us  [decoder_block(): pl.pallas_call(functools.partial(main_kernel, n, head_dim, capacity), out...]
where the time goes in v5:
time: 47.2 us; the launch traced here: 47.1 us
  Pallas kernels  46.5 us (99%)
  between operations  0.65 us (1%)
    pallas_call x1, Pallas kernels, decoder_block(): pl.pallas_call(functools.partial(main_kernel, n, head_dim, capacity), out...  39.9 us
    pallas_call x1, Pallas kernels, decoder_block(): pl.pallas_call(write_kernel, out_shape=(pltpu.HBM((rows, width), BF16), p...  6.6 us

profile of v5, /device:TPU:81, one launch (start us, length us, event | category | flops | bytes accessed | tf_op | source)
XLA Modules:
  0.0 47.1 jit_solution(4621413649820388019)
XLA Ops:
  0.6 39.9 %main_part.1 = (bf16[16,768]{1,0:T(8,128)(2,1)S(1)}, bf16[16,768,384]{2,1,0:T(8,128)(2,1)S(1)}, bf16[16,768,384]{2,1,0:T(8,128)(2,1)S(1)}) custom-call(s32[16]{0:T(128)} %pos_hbm.1, s32[16]{0:T(128)} %eidx_hbm.1, bf16[16,768]{1,0:T(8,128)(2,1)} %hid_hbm.1, f32[768]{0:T(1024)} %ln_hbm.1, f32[768]{0:T(1024)} %lnc_hbm.1, f32[768]{0:T(1024)} %lnf_hbm.1, ...), custom_call_target="tpu_custom_call" | custom-call | tf_op jit(solution)/shard_map/main_part/pallas_call | solution.py:401
  40.5 6.6 %write_part.1 = (bf16[16,768]{1,0:T(8,128)(2,1)}, bf16[16,768,384]{2,1,0:T(8,128)(2,1)}, bf16[16,768,384]{2,1,0:T(8,128)(2,1)}) custom-call(bf16[16,768]{1,0:T(8,128)(2,1)S(1)} %get-tuple-element.9.hid_ref, bf16[16,768,384]{2,1,0:T(8,128)(2,1)S(1)} %get-tuple-element.10.k_ref, bf16[16,768,384]{2,1,0:T(8,128)(2,1)S(1)} %get-tuple-element.11.v_ref), custom_call_target="tpu_custom_call" | custom-call | tf_op jit(solution)/shard_map/write_part/pallas_call | solution.py:430

commit v6 on v5

--- a/solution.py
+++ b/solution.py
@@ -85,7 +85,6 @@
     half = share // 2
     steps = rows // UNROLL
     peers = len(PEERS)
-    pieces = ((0, share), (share, share), (2 * share, half), (2 * share + half, half))
 
     barrier = pltpu.get_barrier_semaphore()
     for peer in PEERS:
@@ -106,30 +105,47 @@
     lane_id = lax.broadcasted_iota(jnp.int32, (1, 128), 1)
     loads[0].wait()
     pl.semaphore_wait(barrier, n - 1)
-    for copy in to_peers(dev, me, xall_ref, x_sem.at[0], x_sem.at[1]):
-        copy.start()
+    right, left, far, sib = dev(1, 0), dev(3, 0), dev(2, 0), dev(0, 1)
+
+    def send_rows(owner, sem, target):
+        remote(xall_ref.at[owner], xall_ref.at[owner], x_sem.at[0], x_sem.at[sem], target).start()
+
+    def rows_over(owner, sem):
+        remote(xall_ref.at[owner], xall_ref.at[owner], x_sem.at[0], x_sem.at[sem], sib).wait_recv()
+        send_rows(owner, 4, sib)
+
+    send_rows(me, 3, far)
+    send_rows(me, 1, right)
+    send_rows(me, 2, left)
+    send_rows(me, 4, sib)
     pltpu.make_async_copy(mine, mine, in_sem.at[5]).wait()
 
-    right, left, far, sib = dev(1, 0), dev(3, 0), dev(2, 0), dev(0, 1)
+    def half_of(owner, part):
+        return wall_ref.at[owner, pl.ds(part * half, half)]
 
     def send_piece(owner, role, part, target):
-        start, size = pieces[part]
-        block = wall_ref.at[owner, pl.ds(start, size)]
         sem = pair_recv.at[part // 2] if role is None else w_recv.at[role, part]
-        remote(block, block, w_send.at[0], sem, target).start()
+        remote(half_of(owner, part), half_of(owner, part), w_send.at[0], sem, target).start()
 
     def wait_piece(owner, role, part):
-        start, size = pieces[part]
-        block = wall_ref.at[owner, pl.ds(start, size)]
-        remote(block, block, w_send.at[0], w_recv.at[role, part], sib).wait_recv()
+        remote(half_of(owner, part), half_of(owner, part), w_send.at[0], w_recv.at[role, part], sib).wait_recv()
 
     def wait_pair(stage):
-        size = 2 * share if stage == 0 else share
-        block = wall_ref.at[pl.ds(0, n // 2), pl.ds(0, size)]
+        block = wall_ref.at[pl.ds(0, n // 2), pl.ds(stage * share, share)]
         remote(block, block, w_send.at[0], pair_recv.at[stage], sib).wait_recv()
 
-    send_piece(me, FROM_LEFT, 0, right)
-    send_piece(me, FROM_RIGHT, 1, left)
+    def pass_on(first):
+        wait_piece(left, FROM_LEFT, first)
+        send_piece(left, FROM_FAR, first, right)
+        wait_piece(right, FROM_RIGHT, first + 1)
+        send_piece(right, FROM_FAR, first + 1, left)
+
+    def send_own(*parts):
+        for part in parts:
+            send_piece(me, FROM_LEFT, part, right)
+            send_piece(me, FROM_RIGHT, part + 1 if part % 2 == 0 else part - 1, left)
+
+    send_own(0, 1, 2)
     loads[1].wait()
     loads[10].wait()
     e_row = jnp.zeros((1, 128), jnp.int32)
@@ -153,10 +169,13 @@
                      + jnp.dot(low, flip, preferred_element_type=F32))
     qsend_ref[...] = jnp.zeros_like(qsend_ref)
 
+    rows_over(left, 1)
+    rows_over(right, 2)
     for load in loads[2:3] + loads[11:]:
         load.wait()
     pltpu.make_async_copy(wqkv_ref, wqkv_ref, in_sem.at[3]).wait()
-    all_of(xall_ref, peers, x_sem.at[0], x_sem.at[1], sib).wait_recv()
+    rows_over(far, 3)
+    all_of(xall_ref, n // 2, x_sem.at[0], x_sem.at[4], sib).wait_recv()
     x_norm = rms_norm(xall_ref[...].reshape(n * rows, width).astype(F32), ln_ref[...][None])
     for part in range(3):
         qsend_ref[:, part * 128:part * 128 + share] = dot_nt(x_norm, wqkv_ref[part]).astype(BF16)
@@ -164,24 +183,29 @@
         dst = dev(*peer)
         remote(qsend_ref.at[pl.ds(dst * rows, rows)], qrecv_ref.at[me], q_sem.at[0], q_sem.at[1], dst).start()
     qrecv_ref[me] = qsend_ref[pl.ds(pl.multiple_of(me * rows, rows), rows), :]
-    send_piece(me, FROM_LEFT, 1, right)
-    send_piece(me, FROM_RIGHT, 0, left)
-    for part in range(len(pieces)):
+    pass_on(0)
+    send_own(3)
+    for part in range(6):
         send_piece(me, None, part, sib)
+
+    all_of(qrecv_ref, peers, q_sem.at[0], q_sem.at[1], sib).wait_recv()
+    def far_over(first):
+        for part in (first, first + 1):
+            wait_piece(far, FROM_FAR, part)
+            send_piece(far, None, part, sib)
+
+    pass_on(2)
+    send_own(4, 5)
     for copy in (to_peers(dev, me, wr_ref, r_sem.at[0], r_sem.at[1])
                  + to_peers(dev, me, eall_ref, e_sem.at[0], e_sem.at[1])):
         copy.start()
-
-    all_of(qrecv_ref, peers, q_sem.at[0], q_sem.at[1], sib).wait_recv()
-    wait_piece(left, FROM_LEFT, 0)
-    send_piece(left, FROM_FAR, 0, right)
-    wait_piece(right, FROM_RIGHT, 1)
-    send_piece(right, FROM_FAR, 1, left)
-    for part in (2, 3):
-        send_piece(me, FROM_LEFT, part, right)
-        send_piece(me, FROM_RIGHT, 5 - part, left)
-    send_piece(left, None, 0, sib)
-    send_piece(right, None, 1, sib)
+    wait_piece(left, FROM_LEFT, 1)
+    wait_piece(right, FROM_RIGHT, 0)
+    for part in (0, 1):
+        send_piece(left, None, part, sib)
+        send_piece(right, None, part, sib)
+    send_piece(left, None, 2, sib)
+    send_piece(right, None, 3, sib)
 
     def columns(part):
         return jnp.concatenate([qrecv_ref[s][:, part * 128:part * 128 + share] for s in range(n)], axis=1).astype(F32)
@@ -221,26 +245,23 @@
             ctx32_ref[pl.ds(b, 1), :] = jnp.sum(spread * h_mask, axis=0, keepdims=True)
         return carry
     lax.fori_loop(0, steps // 2, value_step, 0)
-    for owner, role, part in ((left, FROM_LEFT, 1), (right, FROM_RIGHT, 0)):
-        wait_piece(owner, role, part)
-        send_piece(owner, None, part, sib)
+    far_over(0)
+    wait_piece(left, FROM_LEFT, 3)
+    send_piece(left, None, 3, sib)
+    wait_piece(right, FROM_RIGHT, 2)
+    send_piece(right, None, 2, sib)
     lax.fori_loop(steps // 2, steps, value_step, 0)
 
-    for part in (0, 1):
-        wait_piece(far, FROM_FAR, part)
-        send_piece(far, None, part, sib)
+    far_over(2)
     wait_pair(0)
-
-    wait_piece(left, FROM_LEFT, 2)
-    send_piece(left, FROM_FAR, 2, right)
-    wait_piece(right, FROM_RIGHT, 3)
-    send_piece(right, FROM_FAR, 3, left)
-    send_piece(left, None, 2, sib)
-    send_piece(right, None, 3, sib)
     wo = wall_ref[:, 0:share, :].reshape(width, width)
     h1 = (hid_ref[...].astype(F32) + dot_nt(ctx32_ref[...].astype(BF16), wo)).astype(BF16).astype(F32)
+    wait_pair(1)
     wqc = wall_ref[:, share:2 * share, :].reshape(width, width)
     q_ref[...] = dot_nt(rms_norm(h1, lnc_ref[...][None]), wqc).astype(BF16).astype(F32)
+    pass_on(4)
+    send_piece(left, None, 4, sib)
+    send_piece(right, None, 5, sib)
     for load in big[2:]:
         load.wait()
 
@@ -252,9 +273,10 @@
             s2_ref[b] = jnp.where(mask_ref[pl.ds(b, 1), :] == 1, scores, NEG_BIG)
         return carry
     lax.fori_loop(0, steps, cross_score, 0)
-    for owner, role, part in ((left, FROM_LEFT, 3), (right, FROM_RIGHT, 2)):
-        wait_piece(owner, role, part)
-        send_piece(owner, None, part, sib)
+    wait_piece(left, FROM_LEFT, 5)
+    send_piece(left, None, 5, sib)
+    wait_piece(right, FROM_RIGHT, 4)
+    send_piece(right, None, 4, sib)
     p2_ref[...] = softmax_rows(s2_ref[...])
 
     def cross_value(i, carry):
@@ -265,10 +287,8 @@
         return carry
     lax.fori_loop(0, steps, cross_value, 0)
 
-    for part in (2, 3):
-        wait_piece(far, FROM_FAR, part)
-        send_piece(far, None, part, sib)
-    wait_pair(1)
+    far_over(4)
+    wait_pair(2)
     woc = wall_ref[:, 2 * share:3 * share, :].reshape(width, width)
     h2 = (h1 + dot_nt(ctx32_ref[...].astype(BF16), woc)).astype(BF16).astype(F32)
     x_own = rms_norm(h2, lnf_ref[...][None])
@@ -417,8 +437,8 @@
                 vmem((heads_pad, length), F32), vmem((n * rows, experts * units), BF16),
                 vmem((parts, n // 2, 2, rows, chunk), F32), vmem((parts, n // 2, rows, chunk), F32),
                 vmem((parts, n // 2, rows, chunk), F32), vmem((parts, n // 2, rows, chunk), F32),
-                dma((12,)), dma((6,)), dma((2,)), dma((2,)), dma((2,)), dma((2,)), dma((2,)), dma((1,)), dma((3, 4)),
-                dma((2,)), dma((1,)), dma((parts,)), dma((1,)), dma((parts,)),
+                dma((12,)), dma((6,)), dma((5,)), dma((2,)), dma((2,)), dma((2,)), dma((2,)), dma((1,)), dma((3, 6)),
+                dma((3,)), dma((1,)), dma((parts,)), dma((1,)), dma((parts,)),
             ],
             compiler_params=pltpu.CompilerParams(collective_id=0, has_side_effects=True,
                                                  vmem_limit_bytes=34 * 2 ** 20),

time: 47.2 us -> 45.9 us (0.972)
  Pallas kernels: 46.5 us -> 45.1 us
    pallas_call x1, Pallas kernels: 39.9 us -> 38.5 us  [decoder_block(): pl.pallas_call(functools.partial(main_kernel, n, head_dim, capacity), out...]
where the time goes in v6:
time: 45.9 us; the launch traced here: 45.8 us
  Pallas kernels  45.1 us (98%)
  between operations  0.65 us (1%)
    pallas_call x1, Pallas kernels, decoder_block(): pl.pallas_call(functools.partial(main_kernel, n, head_dim, capacity), out...  38.5 us
    pallas_call x1, Pallas kernels, decoder_block(): pl.pallas_call(write_kernel, out_shape=(pltpu.HBM((rows, width), BF16), p...  6.6 us

profile of v6, /device:TPU:81, one launch (start us, length us, event | category | flops | bytes accessed | tf_op | source)
XLA Modules:
  0.0 45.8 jit_solution(6370085575541386285)
XLA Ops:
  0.6 38.5 %main_part.1 = (bf16[16,768]{1,0:T(8,128)(2,1)S(1)}, bf16[16,768,384]{2,1,0:T(8,128)(2,1)S(1)}, bf16[16,768,384]{2,1,0:T(8,128)(2,1)S(1)}) custom-call(s32[16]{0:T(128)} %pos_hbm.1, s32[16]{0:T(128)} %eidx_hbm.1, bf16[16,768]{1,0:T(8,128)(2,1)} %hid_hbm.1, f32[768]{0:T(1024)} %ln_hbm.1, f32[768]{0:T(1024)} %lnc_hbm.1, f32[768]{0:T(1024)} %lnf_hbm.1, ...), custom_call_target="tpu_custom_call" | custom-call | tf_op jit(solution)/shard_map/main_part/pallas_call | solution.py:421
  39.2 6.6 %write_part.1 = (bf16[16,768]{1,0:T(8,128)(2,1)}, bf16[16,768,384]{2,1,0:T(8,128)(2,1)}, bf16[16,768,384]{2,1,0:T(8,128)(2,1)}) custom-call(bf16[16,768]{1,0:T(8,128)(2,1)S(1)} %get-tuple-element.9.hid_ref, bf16[16,768,384]{2,1,0:T(8,128)(2,1)S(1)} %get-tuple-element.10.k_ref, bf16[16,768,384]{2,1,0:T(8,128)(2,1)S(1)} %get-tuple-element.11.v_ref), custom_call_target="tpu_custom_call" | custom-call | tf_op jit(solution)/shard_map/write_part/pallas_call | solution.py:450

commit v7 on v6

--- a/solution.py
+++ b/solution.py
@@ -15,7 +15,7 @@
 NT = (((1,), (1,)), ((), ()))
 FROM_LEFT, FROM_RIGHT, FROM_FAR = 0, 1, 2
 PEERS = ((2, 0), (2, 1), (1, 0), (3, 0), (1, 1), (3, 1), (0, 1))
-UNROLL = 4
+UNROLL = 8
 
 
 def in_hbm(*arrays):
@@ -256,12 +256,12 @@
     wait_pair(0)
     wo = wall_ref[:, 0:share, :].reshape(width, width)
     h1 = (hid_ref[...].astype(F32) + dot_nt(ctx32_ref[...].astype(BF16), wo)).astype(BF16).astype(F32)
+    pass_on(4)
+    send_piece(left, None, 4, sib)
+    send_piece(right, None, 5, sib)
     wait_pair(1)
     wqc = wall_ref[:, share:2 * share, :].reshape(width, width)
     q_ref[...] = dot_nt(rms_norm(h1, lnc_ref[...][None]), wqc).astype(BF16).astype(F32)
-    pass_on(4)
-    send_piece(left, None, 4, sib)
-    send_piece(right, None, 5, sib)
     for load in big[2:]:
         load.wait()
 
@@ -285,9 +285,10 @@
             spread = dot_nt(p2_ref[b], cv_ref[b])
             ctx32_ref[pl.ds(b, 1), :] = jnp.sum(spread * h_mask, axis=0, keepdims=True)
         return carry
-    lax.fori_loop(0, steps, cross_value, 0)
-
+    lax.fori_loop(0, steps // 2, cross_value, 0)
     far_over(4)
+    lax.fori_loop(steps // 2, steps, cross_value, 0)
+
     wait_pair(2)
     woc = wall_ref[:, 2 * share:3 * share, :].reshape(width, width)
     h2 = (h1 + dot_nt(ctx32_ref[...].astype(BF16), woc)).astype(BF16).astype(F32)

time: 45.9 us -> 44.5 us (0.969)
  Pallas kernels: 45.1 us -> 43.8 us
    pallas_call x1, Pallas kernels: 38.5 us -> 37.2 us  [decoder_block(): pl.pallas_call(functools.partial(main_kernel, n, head_dim, capacity), out...]
where the time goes in v7:
time: 44.5 us; the launch traced here: 44.4 us
  Pallas kernels  43.8 us (98%)
  between operations  0.65 us (1%)
    pallas_call x1, Pallas kernels, decoder_block(): pl.pallas_call(functools.partial(main_kernel, n, head_dim, capacity), out...  37.2 us
    pallas_call x1, Pallas kernels, decoder_block(): pl.pallas_call(write_kernel, out_shape=(pltpu.HBM((rows, width), BF16), p...  6.6 us

profile of v7, /device:TPU:81, one launch (start us, length us, event | category | flops | bytes accessed | tf_op | source)
XLA Modules:
  0.0 44.4 jit_solution(3557801175828789459)
XLA Ops:
  0.6 37.2 %main_part.1 = (bf16[16,768]{1,0:T(8,128)(2,1)S(1)}, bf16[16,768,384]{2,1,0:T(8,128)(2,1)S(1)}, bf16[16,768,384]{2,1,0:T(8,128)(2,1)S(1)}) custom-call(s32[16]{0:T(128)} %pos_hbm.1, s32[16]{0:T(128)} %eidx_hbm.1, bf16[16,768]{1,0:T(8,128)(2,1)} %hid_hbm.1, f32[768]{0:T(1024)} %ln_hbm.1, f32[768]{0:T(1024)} %lnc_hbm.1, f32[768]{0:T(1024)} %lnf_hbm.1, ...), custom_call_target="tpu_custom_call" | custom-call | tf_op jit(solution)/shard_map/main_part/pallas_call | solution.py:422
  37.8 6.6 %write_part.1 = (bf16[16,768]{1,0:T(8,128)(2,1)}, bf16[16,768,384]{2,1,0:T(8,128)(2,1)}, bf16[16,768,384]{2,1,0:T(8,128)(2,1)}) custom-call(bf16[16,768]{1,0:T(8,128)(2,1)S(1)} %get-tuple-element.9.hid_ref, bf16[16,768,384]{2,1,0:T(8,128)(2,1)S(1)} %get-tuple-element.10.k_ref, bf16[16,768,384]{2,1,0:T(8,128)(2,1)S(1)} %get-tuple-element.11.v_ref), custom_call_target="tpu_custom_call" | custom-call | tf_op jit(solution)/shard_map/write_part/pallas_call | solution.py:451

commit v8 on v7

--- a/solution.py
+++ b/solution.py
@@ -9,6 +9,7 @@
 EPSILON = 1e-6
 NEG_BIG = -1e30
 F32, BF16 = jnp.float32, jnp.bfloat16
+BF16_MAX = float(jnp.finfo(jnp.bfloat16).max)
 MESH = pl.DeviceIdType.MESH
 VM = pl.BlockSpec(memory_space=pltpu.VMEM)
 HBM = pl.BlockSpec(memory_space=pltpu.HBM)
@@ -161,7 +162,7 @@
     rel = jnp.concatenate([rel_ref[...], jnp.zeros((heads_pad - rel_ref.shape[0], length), F32)], axis=0)
     flip = (lax.broadcasted_iota(jnp.int32, (length, length), 0) + lax.broadcasted_iota(jnp.int32, (length, length), 1)
             == length - 1).astype(F32).astype(BF16)
-    hi = rel.astype(BF16)
+    hi = jnp.clip(rel, -BF16_MAX, BF16_MAX).astype(BF16)
     rest = rel - hi.astype(F32)
     mid = rest.astype(BF16)
     low = (rest - mid.astype(F32)).astype(BF16)
@@ -242,7 +243,7 @@
             new = jnp.sum(jnp.where(here, probs, 0.0), axis=1, keepdims=True)
             spread = dot_nt(jnp.where(here, 0.0, probs).astype(BF16), v_ref[b])
             spread = spread + new * kv_ref[1, pl.ds(b, 1), :]
-            ctx32_ref[pl.ds(b, 1), :] = jnp.sum(spread * h_mask, axis=0, keepdims=True)
+            ctx32_ref[pl.ds(b, 1), :] = jnp.sum(jnp.where(h_mask > 0, spread, 0.0), axis=0, keepdims=True)
         return carry
     lax.fori_loop(0, steps // 2, value_step, 0)
     far_over(0)
@@ -283,7 +284,7 @@
         for s in range(UNROLL):
             b = i * UNROLL + s
             spread = dot_nt(p2_ref[b], cv_ref[b])
-            ctx32_ref[pl.ds(b, 1), :] = jnp.sum(spread * h_mask, axis=0, keepdims=True)
+            ctx32_ref[pl.ds(b, 1), :] = jnp.sum(jnp.where(h_mask > 0, spread, 0.0), axis=0, keepdims=True)
         return carry
     lax.fori_loop(0, steps // 2, cross_value, 0)
     far_over(4)

time: 44.5 us -> 44.5 us (level)
  no operation moved by 1% of the time
where the time goes in v8:
time: 44.5 us; the launch traced here: 44.4 us
  Pallas kernels  43.8 us (98%)
  between operations  0.65 us (1%)
    pallas_call x1, Pallas kernels, decoder_block(): pl.pallas_call(functools.partial(main_kernel, n, head_dim, capacity), out...  37.2 us
    pallas_call x1, Pallas kernels, decoder_block(): pl.pallas_call(write_kernel, out_shape=(pltpu.HBM((rows, width), BF16), p...  6.6 us

profile of v8, /device:TPU:81, one launch (start us, length us, event | category | flops | bytes accessed | tf_op | source)
XLA Modules:
  0.0 44.4 jit_solution(17464366530269859355)
XLA Ops:
  0.6 37.2 %main_part.1 = (bf16[16,768]{1,0:T(8,128)(2,1)S(1)}, bf16[16,768,384]{2,1,0:T(8,128)(2,1)S(1)}, bf16[16,768,384]{2,1,0:T(8,128)(2,1)S(1)}) custom-call(s32[16]{0:T(128)} %pos_hbm.1, s32[16]{0:T(128)} %eidx_hbm.1, bf16[16,768]{1,0:T(8,128)(2,1)} %hid_hbm.1, f32[768]{0:T(1024)} %ln_hbm.1, f32[768]{0:T(1024)} %lnc_hbm.1, f32[768]{0:T(1024)} %lnf_hbm.1, ...), custom_call_target="tpu_custom_call" | custom-call | tf_op jit(solution)/shard_map/main_part/pallas_call | solution.py:423
  37.8 6.6 %write_part.1 = (bf16[16,768]{1,0:T(8,128)(2,1)}, bf16[16,768,384]{2,1,0:T(8,128)(2,1)}, bf16[16,768,384]{2,1,0:T(8,128)(2,1)}) custom-call(bf16[16,768]{1,0:T(8,128)(2,1)S(1)} %get-tuple-element.9.hid_ref, bf16[16,768,384]{2,1,0:T(8,128)(2,1)S(1)} %get-tuple-element.10.k_ref, bf16[16,768,384]{2,1,0:T(8,128)(2,1)S(1)} %get-tuple-element.11.v_ref), custom_call_target="tpu_custom_call" | custom-call | tf_op jit(solution)/shard_map/write_part/pallas_call | solution.py:452
